TPU v7x, 128 devices: a whole 4x4x4 slice. The times are simulated.
128 devices in a mesh: ez: 4 (over z), ey: 4 (over y), ex: 8 (over x, core).
Axes of the slice: x: 4, y: 4, z: 4, core: 2. Of those that a mesh axis runs over, the one named last changes fastest.
Arguments:
- x_tokens: bfloat16 [16384, 2048], P(('ez', 'ey', 'ex'))
- expert_ids: int32 [16384, 8], P(('ez', 'ey', 'ex'))
- gate_vals: float32 [16384, 8], P(('ez', 'ey', 'ex'))
- w_gate: bfloat16 [128, 2048, 768], P(('ex', 'ey', 'ez'))
- w_up: bfloat16 [128, 2048, 768], P(('ex', 'ey', 'ez'))
- w_down: bfloat16 [128, 768, 2048], P(('ex', 'ey', 'ez'))
Outputs:
- output: bfloat16 [16384, 2048], P(('ez', 'ey', 'ex'))
All inputs are finite; a program needn't handle non-finite values.
Results may differ from a plain program's by a relative error of at most 0.00512202.
Values are sent between devices in bfloat16 or wider.
A program may use at most 1 GiB of HBM per device.

v0:
```python
import jax
import jax.numpy as jnp
from jax import lax
from jax.sharding import PartitionSpec as P

TOKEN_AXES = ('ez', 'ey', 'ex')
EXPERT_AXES = ('ex', 'ey', 'ez')


def slot_layout(ids_local, n_exp, cap_slot):
    tok_dev, top_k = ids_local.shape
    flat_ids = ids_local.reshape(-1)
    match_mat = (flat_ids[:, None] == jnp.arange(n_exp)[None, :]).astype(jnp.int32)
    slot_rank = jnp.sum(jnp.cumsum(match_mat, axis=0) * match_mat, axis=1) - 1
    slot_idx = flat_ids * cap_slot + slot_rank
    pair_tok = jnp.arange(tok_dev * top_k, dtype=jnp.int32) // top_k
    slot_tok = jnp.zeros((n_exp * cap_slot,), jnp.int32).at[slot_idx].set(pair_tok)
    return slot_idx, slot_tok


def solution(mesh):
    n_dev = mesh.shape['ez'] * mesh.shape['ey'] * mesh.shape['ex']

    def local_layer(x_loc, ids_loc, gates_loc, w_g, w_u, w_d):
        tok_dev, hid_dim = x_loc.shape
        top_k = ids_loc.shape[1]
        n_local = w_g.shape[0]
        n_exp = n_local * n_dev
        cap_slot = 2 * tok_dev * top_k // n_exp
        slot_idx, slot_tok = slot_layout(ids_loc, n_exp, cap_slot)
        send_buf = jnp.take(x_loc, slot_tok, axis=0).reshape(n_dev, n_local, cap_slot, hid_dim)
        recv_buf = lax.all_to_all(send_buf, EXPERT_AXES, 0, 0)
        h_gate = jnp.einsum('slch,lhf->slcf', recv_buf, w_g, preferred_element_type=jnp.float32)
        h_up = jnp.einsum('slch,lhf->slcf', recv_buf, w_u, preferred_element_type=jnp.float32)
        act_bf = (jax.nn.silu(h_gate) * h_up).astype(jnp.bfloat16)
        exp_out = jnp.einsum('slcf,lfh->slch', act_bf, w_d, preferred_element_type=jnp.float32).astype(jnp.bfloat16)
        back_buf = lax.all_to_all(exp_out, EXPERT_AXES, 0, 0)
        back_flat = back_buf.reshape(n_exp * cap_slot, hid_dim)
        tok_rows = jnp.take(back_flat, slot_idx, axis=0).reshape(tok_dev, top_k, hid_dim)
        moe_sum = jnp.sum(gates_loc[:, :, None] * tok_rows, axis=1)
        return (x_loc.astype(jnp.float32) + moe_sum).astype(jnp.bfloat16)

    tok_spec = P(TOKEN_AXES, None)
    w_spec = P(EXPERT_AXES, None, None)
    return jax.shard_map(local_layer, mesh=mesh, in_specs=(tok_spec, tok_spec, tok_spec, w_spec, w_spec, w_spec), out_specs=tok_spec, check_vma=False)
```

profile of v0, /device:TPU:1, one launch (start us, length us, event | category | flops | bytes accessed | tf_op | source)
XLA Modules:
  0.0 357.5 jit_solution(387520190839851293)
XLA Ops:
  0.0 0.9 copy.28
  1.1 0.7 broadcast_multiply_fusion
  1.8 0.1 copy.30
  1.9 0.2 fusion.24
  2.1 0.8 copy-done.3
  3.0 1.1 broadcast_add_fusion
  4.0 0.1 copy.31
  4.1 0.4 fusion.23
  4.5 0.1 copy.34
  4.7 4.3 %scatter_custom_fusion = s32[2048]{0:T(1024)S(1)} fusion(s32[1024]{0:T(1024)S(1)} %bitcast.85, s32[1024]{0:T(1024)S(1)} %add_select_fusion, s32[]{:T(128)} %constant.52.clone.1), kind=kCustom, calls=%fused_computation.45 | custom fusion | bytes 8196 | tf_op jit(solution)/shard_map/scatter | solution.py:17
  9.2 17.4 %gather_fusion = bf16[2048,2048]{1,0:T(8,128)(2,1)} fusion(bf16[128,2048]{1,0:T(8,128)(2,1)} %param.6, s32[2048]{0:T(1024)S(1)} %fusion.27), kind=kCustom, calls=%fused_computation | custom fusion | bytes 16785408 | tf_op jit(solution)/shard_map/jit(_take)/gather | solution.py:31
  26.6 7.4 %select_bitcast_fusion = bf16[128,1,16,2048]{3,2,1,0:T(8,128)(2,1)} fusion(bf16[128,1,16,2048]{3,2,0,1:T(8,128)(2,1)} %bitcast.83, pred[128,16]{1,0:T(8,128)(4,1)S(1)} %broadcast_in_dim.32), kind=kLoop, calls=%fused_computation.9 | loop fusion | flops 4194304 | bytes 16779264 | tf_op jit(solution)/shard_map/jit(_take)/select_n | solution.py:31
  34.1 121.1 %all_to_all.10 = bf16[128,1,16,2048]{3,2,1,0:T(8,128)(2,1)S(1)} all-to-all(bf16[128,1,16,2048]{3,2,1,0:T(8,128)(2,1)} %select_bitcast_fusion), channel_id=1, replica_groups=mesh['ez'=4,'ey'=4,'ex'=8] {'ex','ey','ez'}, dimensions={0} | all-to-all | bytes 16777216 | tf_op jit(solution)/shard_map/all_to_all | solution.py:32
  155.2 3.2 copy-done.2
  158.4 17.6 %fusion = f32[128,16,768]{2,0,1:T(8,128)} fusion(bf16[128,1,16,2048]{3,2,1,0:T(8,128)(2,1)S(1)} %all_to_all.10, bf16[1,2048,768]{2,1,0:T(8,128)(2,1)S(1)} %copy-done.6), kind=kOutput, calls=%fused_computation.3 | convolution fusion | flops 6442450944 | bytes 17825792 | tf_op jit(solution)/shard_map/slch,lhf->slcf/dot_general | solution.py:34
  176.0 25.9 %convert_bitcast_fusion = bf16[128,1,16,2048]{3,0,2,1:T(8,128)(2,1)} fusion(bf16[1,768,2048]{2,1,0:T(8,128)(2,1)S(1)} %copy-done, f32[128,16,768]{2,0,1:T(8,128)} %fusion, bf16[128,1,16,2048]{3,2,1,0:T(8,128)(2,1)} %copy-done.2, bf16[1,2048,768]{2,1,0:T(8,128)(2,1)} %param.9), kind=kOutput, calls=%fused_computation.8 | convolution fusion | flops 12898533376 | bytes 29360128 | tf_op jit(solution)/shard_map/slcf,lfh->slch/dot_general | solution.py:36
  201.9 11.2 %copy.37 = bf16[128,1,16,2048]{3,2,1,0:T(8,128)(2,1)} copy(bf16[128,1,16,2048]{3,0,2,1:T(8,128)(2,1)} %convert_bitcast_fusion) | data formatting | bytes 16777216 | tf_op jit(solution)/shard_map/convert_element_type | solution.py:36
  213.1 10.8 %all-to-all-start.1 = ((bf16[128,1,16,2048]{3,2,1,0:T(8,128)(2,1)}), bf16[128,1,16,2048]{3,2,1,0:T(8,128)(2,1)}, u32[]{:S(2)}, u32[]{:S(2)}) async-start(bf16[128,1,16,2048]{3,2,1,0:T(8,128)(2,1)} %copy.37), calls=%async_computation.1 | async-start | bytes 16777216 | tf_op jit(solution)/shard_map/all_to_all | solution.py:37
  224.1 0.1 copy.33
  224.3 0.1 copy.27
  224.4 112.1 %all-to-all-done.1 = bf16[128,1,16,2048]{3,2,1,0:T(8,128)(2,1)} async-done(((bf16[128,1,16,2048]{3,2,1,0:T(8,128)(2,1)}), bf16[128,1,16,2048]{3,2,1,0:T(8,128)(2,1)}, u32[]{:S(2)}, u32[]{:S(2)}) %all-to-all-start.1) | async-done | bytes 8388640 | tf_op jit(solution)/shard_map/all_to_all | solution.py:37
  336.5 13.4 %gather_fusion.1 = bf16[1024,2048]{1,0:T(8,128)(2,1)} fusion(bf16[2048,2048]{1,0:T(8,128)(2,1)} %bitcast.26, s32[1024]{0:T(1024)S(1)} %broadcast_clamp_fusion), kind=kCustom, calls=%fused_computation.1 | custom fusion | bytes 8392704 | tf_op jit(solution)/shard_map/jit(_take)/gather | solution.py:39
  349.9 5.6 %multiply_reduce_fusion = f32[128,2048]{1,0:T(8,128)S(1)} fusion(bf16[1024,2048]{1,0:T(8,128)(2,1)} %gather_fusion.1, f32[128,8]{1,0:T(8,128)S(1)} %copy.27, pred[128,8]{1,0:T(8,128)(4,1)S(1)} %copy.33), kind=kLoop, calls=%fused_computation.7 | loop fusion | flops 8126464 | bytes 5248000 | tf_op jit(solution)/shard_map/reduce_sum | solution.py:40
  355.5 2.0 add_convert_fusion
  (28 shorter events, 0.6 us)
Async XLA Ops:
  0.0 176.0 %copy-start = (bf16[1,768,2048]{2,1,0:T(8,128)(2,1)S(1)}, bf16[1,768,2048]{2,1,0:T(8,128)(2,1)}, u32[]{:S(2)}) copy-start(bf16[1,768,2048]{2,1,0:T(8,128)(2,1)} %param.11) | copy-start | bytes 9437188
  2.1 0.8 copy-start.3
  34.1 124.3 %copy-start.6 = (bf16[1,2048,768]{2,1,0:T(8,128)(2,1)S(1)}, bf16[1,2048,768]{2,1,0:T(8,128)(2,1)}, u32[]{:S(2)}) copy-start(bf16[1,2048,768]{2,1,0:T(8,128)(2,1)} %param.10) | copy-start | bytes 9437188
  155.2 3.2 copy-start.2
  213.1 11.0 %copy-start.4 = (s32[128,8]{0,1:T(8,128)S(1)}, s32[128,8]{0,1:T(8,128)}, u32[]{:S(2)}) copy-start(s32[128,8]{0,1:T(8,128)} %param.7) | copy-start | bytes 12292
  213.1 11.1 %copy-start.5 = (f32[128,8]{0,1:T(8,128)S(1)}, f32[128,8]{0,1:T(8,128)}, u32[]{:S(2)}) copy-start(f32[128,8]{0,1:T(8,128)} %param.8) | copy-start | bytes 12292
  213.1 123.3 %all-to-all-start.1 = ((bf16[128,1,16,2048]{3,2,1,0:T(8,128)(2,1)}), bf16[128,1,16,2048]{3,2,1,0:T(8,128)(2,1)}, u32[]{:S(2)}, u32[]{:S(2)}) async-start(bf16[128,1,16,2048]{3,2,1,0:T(8,128)(2,1)} %copy.37), calls=%async_computation.1 | async-start | bytes 16777216 | tf_op jit(solution)/shard_map/all_to_all | solution.py:37
  336.5 21.0 %copy-start.1 = (bf16[1,768,2048]{2,1,0:T(8,128)(2,1)S(1)}, bf16[1,768,2048]{2,1,0:T(8,128)(2,1)}, u32[]{:S(2)}) copy-start(bf16[1,768,2048]{2,1,0:T(8,128)(2,1)} %param.11) | copy-start | bytes 9437188
where the time goes:
time: 358 us; the launch traced here: 357 us
  blocking collectives  121 us (34%)
  waiting for transfers between devices  112 us (31%)
  local copies, waits for them, and re-layouts  52.4 us (15%)
  matrix products  43.5 us (12%)
  other arithmetic  17.4 us (5%)
  starting transfers between devices  10.8 us (3%)
    all_to_all x1, blocking collectives, local_layer(): recv_buf = lax.all_to_all(send_buf, EXPERT_AXES, 0, 0)  121 us
    all_to_all x1, waiting for transfers between devices, local_layer(): back_buf = lax.all_to_all(exp_out, EXPERT_AXES, 0, 0)  112 us
    dot_general x1, matrix products, local_layer(): jnp.einsum('slcf,lfh->slch', act_bf, w_d, preferred_element_type=jnp.floa...  25.9 us
    dot_general x1, matrix products, local_layer(): jnp.einsum('slch,lhf->slcf', recv_buf, w_u, preferred_element_type=jnp.fl...  17.6 us
    gather x1, local copies, waits for them, and re-layouts, local_layer(): jnp.take(x_loc, slot_tok, axis=0).reshape(n_dev, n_local, cap_slot, hid_dim)  17.4 us
    gather x1, local copies, waits for them, and re-layouts, local_layer(): jnp.take(back_flat, slot_idx, axis=0).reshape(tok_dev, top_k, hid_dim)  13.4 us
    convert_element_type x1, local copies, waits for them, and re-layouts, local_layer(): jnp.einsum('slcf,lfh->slch', act_bf, w_d, preferred_element_type=jnp.floa...  11.2 us
    all_to_all x1, starting transfers between devices, local_layer(): back_buf = lax.all_to_all(exp_out, EXPERT_AXES, 0, 0)  10.8 us
  transfers between devices with their start and end apart: 1, of which 1 were waited for; matrix products, arithmetic and copies ran while one was open for 0% of the time, Pallas kernels for 0%

commit v1 on v0

v1 whole, which is shorter than its diff:
```python
import functools

import jax
import jax.numpy as jnp
from jax import lax
from jax.experimental import pallas as pl
from jax.experimental.pallas import tpu as pltpu
from jax.sharding import PartitionSpec as P

TOKEN_AXES = ('ez', 'ey', 'ex')
EXPERT_AXES = ('ex', 'ey', 'ez')
MESH = pl.DeviceIdType.MESH
F32 = jnp.float32
BF16 = jnp.bfloat16

Z, Y, X = 0, 1, 2
D1 = (Y, Z, X)
D2 = (Z, X, Y)
D3 = (X, Y, Z)
A_IS_D1 = (True, False, True)
RING = 4
CORES = 2
CAP = 16
TOK = 128
LEAD = (CORES, RING, RING, RING)


def split_width(hid):
    tiles = hid // 128
    first = -(-tiles // 3)
    rest = tiles - first
    return (first * 128, (rest - rest // 2) * 128, (rest // 2) * 128)


def moe_kernel(widths, fdim, f_tile, x_ref, meta_ref, w1_hbm, w3_hbm, w2_hbm, y_ref, *scr):
    it = iter(scr)
    take3 = lambda: [next(it) for _ in range(3)]
    gat, til, rec = take3(), take3(), take3()
    meta, sel, comb = take3(), take3(), take3()
    pas3, pas4, pas5 = take3(), take3(), take3()
    part, prec, pas6 = take3(), take3(), take3()
    w1, w3, w2, act = next(it), next(it), next(it), next(it)
    send_sem, recv_sem, w_sem, credit = next(it), next(it), next(it), next(it)

    offs = (0, widths[0], widths[0] + widths[1])
    ez, ey, ex = lax.axis_index('ez'), lax.axis_index('ey'), lax.axis_index('ex')
    core = lax.rem(ex, CORES)
    pos = (ez, ey, ex // CORES)
    mod = lambda v: lax.rem(v + RING, RING)
    other = 1 - core

    def peer(dim, off, c):
        q = [mod(pos[d] + off) if d == dim else pos[d] for d in range(3)]
        return (q[0], q[1], q[2] * CORES + c)

    counter = [0]

    def rcopy(src, dst, dev):
        i = counter[0]
        counter[0] += 1
        return pltpu.make_async_remote_copy(src, dst, send_sem.at[i], recv_sem.at[i], device_id=dev, device_id_type=MESH)

    bar = pltpu.get_barrier_semaphore()
    npeer = 0
    for dim in range(3):
        for off in (1, -1):
            for c in (core, other):
                pl.semaphore_signal(bar, inc=1, device_id=peer(dim, off, c), device_id_type=MESH)
                npeer += 1
    pl.semaphore_signal(bar, inc=1, device_id=peer(0, 0, other), device_id_type=MESH)
    w_copies = [pltpu.make_async_copy(s, d, w_sem.at[i]) for i, (s, d) in enumerate(((w1_hbm, w1), (w3_hbm, w3), (w2_hbm, w2)))]
    pl.semaphore_wait(bar, npeer + 1)

    DIRS = (1, -1)
    p1 = [pos[D1[k]] for k in range(3)]
    p2 = [pos[D2[k]] for k in range(3)]
    p3 = [pos[D3[k]] for k in range(3)]

    def chunk(k, r):
        return gat[k].at[:, :, p2[k], mod(p1[k] + r)]

    g1 = [[None, None] for _ in range(3)]
    m1 = [[None, None] for _ in range(3)]
    for k in range(3):
        xk = x_ref.at[:, :, :, pl.ds(offs[k], widths[k])]
        for i, d in enumerate(DIRS):
            m1[k][i] = rcopy(meta_ref, meta[k].at[p2[k], p1[k]], peer(D1[k], d, core))
            m1[k][i].start()
            g1[k][i] = rcopy(xk, chunk(k, 0), peer(D1[k], d, core))
            g1[k][i].start()
    g2 = [[[None] * 4, [None] * 4] for _ in range(3)]
    for k in range(3):
        xk = x_ref.at[:, :, :, pl.ds(offs[k], widths[k])]
        for i, d in enumerate(DIRS):
            g2[k][i][0] = rcopy(xk, chunk(k, 0), peer(D2[k], d, core))
            g2[k][i][0].start()
    for c in w_copies:
        c.start()
    for k in range(3):
        gat[k][:, :, p2[k], p1[k]] = x_ref[:, :, :, offs[k]:offs[k] + widths[k]]
        meta[k][p2[k], p1[k]] = meta_ref[...]
    f1 = [[None, None] for _ in range(3)]
    mf1 = [None] * 3
    for k in range(3):
        for i, d in enumerate(DIRS):
            m1[k][i].wait_recv()
            if i == 0:
                src = meta[k].at[p2[k], mod(p1[k] - 1)]
                mf1[k] = rcopy(src, src, peer(D1[k], 1, core))
                mf1[k].start()
            g1[k][i].wait_recv()
            half = chunk(k, -d).at[i]
            f1[k][i] = rcopy(half, half, peer(D1[k], d, core))
            f1[k][i].start()
    m2 = [[None, None] for _ in range(3)]
    for k in range(3):
        for i, d in enumerate(DIRS):
            for r in (1, 3):
                g2[k][i][r] = rcopy(chunk(k, r), chunk(k, r), peer(D2[k], d, core))
                g2[k][i][r].start()
    for k in range(3):
        mf1[k].wait_recv()
        for i, d in enumerate(DIRS):
            row = meta[k].at[p2[k]]
            m2[k][i] = rcopy(row, row, peer(D2[k], d, core))
            m2[k][i].start()

    def forward2(k, i, r):
        d = DIRS[i]
        g2[k][i][r].wait_recv()
        src = gat[k].at[:, :, mod(p2[k] - d), mod(p1[k] + r)]
        c = rcopy(src, src, peer(D2[k], d, core))
        c.start()
        return c

    f2 = [[None] * 4 for _ in range(3)]
    for k in range(3):
        f2[k][0] = forward2(k, 0, 0)
    for k in range(3):
        for i in range(2):
            f1[k][i].wait_recv()
        for i, d in enumerate(DIRS):
            g2[k][i][2] = rcopy(chunk(k, 2), chunk(k, 2), peer(D2[k], d, core))
            g2[k][i][2].start()
    mf2 = [None] * 3
    for k in range(3):
        for i in range(2):
            m2[k][i].wait_recv()
        src = meta[k].at[mod(p2[k] - 1)]
        mf2[k] = rcopy(src, src, peer(D2[k], 1, core))
        mf2[k].start()
    for k in range(3):
        f2[k][1] = forward2(k, 0, 1)
        f2[k][3] = forward2(k, 1, 3)

    tri = (lax.broadcasted_iota(jnp.int32, (TOK, TOK), 0) < lax.broadcasted_iota(jnp.int32, (TOK, TOK), 1)).astype(BF16)
    i8 = lax.broadcasted_iota(jnp.int32, (8, 1), 0)
    stride3 = (2 * RING * RING, RING, 1)
    strides = (1, RING, 2 * RING * RING)
    slot = lax.broadcasted_iota(jnp.int32, (8, CAP, TOK), 1).astype(F32)

    def experts8(k):
        base = pos[D1[k]] * strides[D1[k]] + pos[D2[k]] * strides[D2[k]]
        return (base + (i8 & 3) * stride3[k] + (i8 >> 2) * (RING * RING)).astype(F32)

    def picked(ids, evec):
        m = (ids[0:1, :] == evec).astype(F32)
        for j in range(1, 8):
            m = m + (ids[j:j + 1, :] == evec).astype(F32)
        return m

    def rank_of(m):
        rank = jnp.dot(m.astype(BF16), tri, preferred_element_type=F32)
        return jnp.where(m > 0.5, rank, -1.0)

    for k in range(3):
        mf2[k].wait_recv()
        evec = experts8(k)

        def ranks(i, carry, k=k, evec=evec):
            rows = [picked(meta[k][i, j, 0:8], evec) for j in range(4)]
            rm = rank_of(jnp.concatenate(rows, axis=0))
            for j in range(4):
                hot = (rm[j * 8:(j + 1) * 8][:, None, :] == slot).astype(F32)
                sel[k][i, j] = hot.reshape(TOK, TOK).astype(BF16)
            return carry

        lax.fori_loop(0, 4, ranks, 0)

    for k in range(3):
        f2[k][2] = forward2(k, 1, 2)

    def sub(ref, k, c, d, half=None):
        a = slice(None) if half is None else pl.ds(2 * half, 2)
        return (ref.at[c, d, a], ref.at[c, a, d], ref.at[c, a, :, d])[k]

    def opened(k):
        for r in (0, 1, 2, 3):
            for i in range(2):
                if (i, r) not in ((0, 0), (0, 1), (1, 3), (1, 2)):
                    g2[k][i][r].wait_recv()
            f2[k][r].wait_recv()
        for c in m1[k] + g1[k] + f1[k] + [mf1[k]] + m2[k] + [mf2[k]] + g2[k][0] + g2[k][1] + f2[k]:
            c.wait_send()

    def exchange_start(k, cr, src, src_block, dst, dst_block, pas, self_copy):
        c = core if cr == 0 else other
        first, direct = [], []
        for i, d in enumerate(DIRS):
            cp = rcopy(src_block(src, c, mod(p3[k] + 2), i), pas.at[i, cr], peer(D3[k], d, core))
            cp.start()
            first.append(cp)
        for i, d in enumerate(DIRS):
            cp = rcopy(src_block(src, c, mod(p3[k] + d), None), dst_block(dst, core, p3[k], None), peer(D3[k], d, c))
            cp.start()
            direct.append(cp)
        if cr == 0:
            self_copy()
        else:
            cp = rcopy(src_block(src, c, p3[k], None), dst_block(dst, core, p3[k], None), peer(D3[k], 0, other))
            cp.start()
            direct.append(cp)
        return first, direct

    def exchange_forward(k, cr, first, direct, dst, dst_block, pas):
        c = core if cr == 0 else other
        for i, d in enumerate(DIRS):
            first[i].wait_recv()
            cp = rcopy(pas.at[i, cr], dst_block(dst, core, mod(p3[k] - d), i), peer(D3[k], d, c))
            cp.start()
            direct.append(cp)

    def til_block(ref, c, d, half):
        return ref.at[c, d] if half is None else ref.at[c, d, pl.ds(2 * half, 2)]

    x3 = [[None, None] for _ in range(3)]
    for k in range(3):
        opened(k)
        w = widths[k]

        def select(i, carry, k=k, w=w):
            for j in range(4):
                rows = gat[k][:, :, i, j].reshape(TOK, w)
                out = jnp.dot(sel[k][i, j], rows, preferred_element_type=F32).astype(BF16).reshape(CORES, RING, CAP, w)
                if A_IS_D1[k]:
                    til[k][:, :, j, i] = out
                else:
                    til[k][:, :, i, j] = out
            return carry

        lax.fori_loop(0, 4, select, 0)
        for cr in range(2):
            def keep(k=k):
                v = til[k][core, p3[k]]
                if k == 0:
                    rec[k][core, p3[k]] = v
                elif k == 1:
                    rec[k][core, :, p3[k]] = v
                else:
                    rec[k][core, :, :, p3[k]] = v
            rblock = lambda ref, c, d, half, k=k: sub(ref, k, c, d, half)
            x3[k][cr] = exchange_start(k, cr, til[k], til_block, rec[k], rblock, pas3[k], keep)
    for k in range(3):
        rblock = lambda ref, c, d, half, k=k: sub(ref, k, c, d, half)
        for cr in range(2):
            exchange_forward(k, cr, *x3[k][cr], rec[k], rblock, pas3[k])
    for k in range(3):
        for cr in range(2):
            first, direct = x3[k][cr]
            for cp in direct:
                cp.wait_recv()
            for cp in first + direct:
                cp.wait_send()
    for c in w_copies:
        c.wait()

    x4 = [[None, None] for _ in range(3)]
    for cr in range(2):
        c = core if cr == 0 else other

        def rows_step(i, carry, c=c):
            rows = 2 * RING * RING * CAP
            xs = [rec[k][c, pl.ds(2 * i, 2)].reshape(rows, widths[k]) for k in range(3)]

            for f in range(fdim // f_tile):
                cols = slice(f * f_tile, (f + 1) * f_tile)
                hg = sum(jnp.dot(xs[k], w1[offs[k]:offs[k] + widths[k], cols], preferred_element_type=F32) for k in range(3))
                hu = sum(jnp.dot(xs[k], w3[offs[k]:offs[k] + widths[k], cols], preferred_element_type=F32) for k in range(3))
                act[:, cols] = (hg * jax.nn.sigmoid(hg) * hu).astype(BF16)
            a = act[...]
            for k in range(3):
                o = jnp.dot(a, w2[:, offs[k]:offs[k] + widths[k]], preferred_element_type=F32).astype(BF16)
                til[k][c, pl.ds(2 * i, 2)] = o.reshape(2, RING, RING, CAP, widths[k])
            return carry

        lax.fori_loop(0, 2, rows_step, 0)
        for k in range(3):
            def keep(k=k):
                if k == 0:
                    v = til[k][core, p3[k]]
                elif k == 1:
                    v = til[k][core, :, p3[k]]
                else:
                    v = til[k][core, :, :, p3[k]]
                gat[k][core, p3[k]] = v
            sblock = lambda ref, cc, d, half, k=k: sub(ref, k, cc, d, half)
            x4[k][cr] = exchange_start(k, cr, til[k], sblock, gat[k], til_block, pas4[k], keep)
    for k in range(3):
        for i, d in enumerate(DIRS):
            pl.semaphore_signal(credit.at[k, i], inc=1, device_id=peer(D1[k], d, core), device_id_type=MESH)
    for cr in range(2):
        for k in range(3):
            exchange_forward(k, cr, *x4[k][cr], gat[k], til_block, pas4[k])

    for k in range(3):
        def weights(i, carry, k=k):
            mrow = meta[k][i, p1[k]]
            ids, gates = mrow[0:8], mrow[8:16]
            own = pos[D2[k]] * strides[D2[k]]
            ms, gs = [], []
            for b in range(4):
                idx = i8 + b * 8
                d3e, d1e, ce = idx & 3, (idx >> 2) & 3, idx >> 4
                evec = (own + d3e * stride3[k] + d1e * strides[D1[k]] + ce * (RING * RING)).astype(F32)
                m = jnp.zeros((8, TOK), F32)
                g = jnp.zeros((8, TOK), F32)
                for j in range(8):
                    hit = ids[j:j + 1, :] == evec
                    m = m + hit.astype(F32)
                    g = g + jnp.where(hit, gates[j:j + 1, :], 0.0)
                ms.append(m)
                gs.append(g)
            rm = rank_of(jnp.concatenate(ms, axis=0))
            for b in range(4):
                hot = jnp.where(rm[b * 8:(b + 1) * 8][:, None, :] == slot, gs[b][:, None, :], 0.0).reshape(TOK, TOK).T
                hi = hot.astype(BF16)
                r1 = hot - hi.astype(F32)
                mid = r1.astype(BF16)
                lo = (r1 - mid.astype(F32)).astype(BF16)
                comb[k][i, b, 0] = hi
                comb[k][i, b, 1] = mid
                comb[k][i, b, 2] = lo
            return carry

        lax.fori_loop(0, 4, weights, 0)

    def from_src(ref, k, d, half=None):
        cs = slice(None) if half is None else half
        return ref.at[cs, :, d] if A_IS_D1[k] else ref.at[cs, :, :, d]

    x5 = [None] * 3
    for k in range(3):
        for cr in range(2):
            first, direct = x4[k][cr]
            for cp in direct:
                cp.wait_recv()
        for i in range(2):
            pl.semaphore_wait(credit.at[k, i], 1)
        first, direct = [], []
        for i, d in enumerate(DIRS):
            cp = rcopy(from_src(gat[k], k, mod(p1[k] + 2), i), pas5[k].at[i], peer(D1[k], d, core))
            cp.start()
            first.append(cp)
        for i, d in enumerate(DIRS):
            cp = rcopy(from_src(gat[k], k, mod(p1[k] + d)), rec[k].at[:, p1[k]], peer(D1[k], d, core))
            cp.start()
            direct.append(cp)
        if A_IS_D1[k]:
            rec[k][:, p1[k]] = gat[k][:, :, p1[k]]
        else:
            rec[k][:, p1[k]] = gat[k][:, :, :, p1[k]]
        x5[k] = (first, direct)
    for k in range(3):
        first, direct = x5[k]
        for i, d in enumerate(DIRS):
            first[i].wait_recv()
            cp = rcopy(pas5[k].at[i], rec[k].at[i, mod(p1[k] - d)], peer(D1[k], d, core))
            cp.start()
            direct.append(cp)

    x6 = [None] * 3
    for k in range(3):
        first, direct = x5[k]
        for cp in direct:
            cp.wait_recv()
        w = widths[k]

        def combine(i, carry, k=k, w=w):
            acc = jnp.zeros((TOK, w), F32)
            for b in range(4):
                o = rec[k][b // 2, pl.ds(2 * (b % 2), 2), :, i].reshape(TOK, w)
                for q in range(3):
                    acc = acc + jnp.dot(comb[k][i, b, q], o, preferred_element_type=F32)
            part[k][i] = acc
            return carry

        lax.fori_loop(0, 4, combine, 0)
        first, direct = [], []
        for i, d in enumerate(DIRS):
            cp = rcopy(part[k].at[mod(p2[k] + 2), pl.ds(i * (TOK // 2), TOK // 2)], pas6[k].at[i], peer(D2[k], d, core))
            cp.start()
            first.append(cp)
        for i, d in enumerate(DIRS):
            cp = rcopy(part[k].at[mod(p2[k] + d)], prec[k].at[i], peer(D2[k], d, core))
            cp.start()
            direct.append(cp)
        x6[k] = (first, direct)
    for k in range(3):
        first, direct = x6[k]
        for i, d in enumerate(DIRS):
            first[i].wait_recv()
            cp = rcopy(pas6[k].at[i], prec[k].at[2, pl.ds(i * (TOK // 2), TOK // 2)], peer(D2[k], d, core))
            cp.start()
            direct.append(cp)
    for k in range(3):
        first, direct = x6[k]
        for cp in direct:
            cp.wait_recv()
        total = part[k][p2[k]] + prec[k][0] + prec[k][1] + prec[k][2]
        xk = x_ref[:, :, :, offs[k]:offs[k] + widths[k]].reshape(TOK, widths[k]).astype(F32)
        y_ref[:, offs[k]:offs[k] + widths[k]] = (xk + total).astype(BF16)
    for k in range(3):
        for cp in x4[k][0][0] + x4[k][0][1] + x4[k][1][0] + x4[k][1][1] + x5[k][0] + x5[k][1] + x6[k][0] + x6[k][1]:
            cp.wait_send()


N_COPIES = 3 * (7 + 15 + 14 + 14 + 6 + 6)


def solution(mesh):
    def local_layer(x_loc, ids_loc, gates_loc, w_g, w_u, w_d):
        tok, hid = x_loc.shape
        fdim = w_g.shape[2]
        widths = split_width(hid)
        f_tile = 256 if fdim % 256 == 0 else fdim
        meta = jnp.concatenate([ids_loc.T.astype(F32), gates_loc.T], axis=0)
        x4 = x_loc.reshape(CORES, RING, CAP, hid)
        scratch = []
        each = lambda f: scratch.extend(f(w) for w in widths)
        for _ in range(3):
            each(lambda w: pltpu.VMEM(LEAD + (CAP, w), BF16))
        each(lambda w: pltpu.VMEM((RING, RING, 16, TOK), F32))
        each(lambda w: pltpu.VMEM((RING, RING, TOK, TOK), BF16))
        each(lambda w: pltpu.VMEM((RING, 4, 3, TOK, TOK), BF16))
        each(lambda w: pltpu.VMEM((2, CORES, 2, RING, CAP, w), BF16))
        each(lambda w: pltpu.VMEM((2, CORES, 2, RING, CAP, w), BF16))
        each(lambda w: pltpu.VMEM((2, RING, RING, CAP, w), BF16))
        each(lambda w: pltpu.VMEM((RING, TOK, w), F32))
        each(lambda w: pltpu.VMEM((3, TOK, w), F32))
        each(lambda w: pltpu.VMEM((2, TOK // 2, w), F32))
        scratch += [
            pltpu.VMEM((hid, fdim), BF16),
            pltpu.VMEM((hid, fdim), BF16),
            pltpu.VMEM((fdim, hid), BF16),
            pltpu.VMEM((2 * RING * RING * CAP, fdim), BF16),
            pltpu.SemaphoreType.DMA((N_COPIES,)),
            pltpu.SemaphoreType.DMA((N_COPIES,)),
            pltpu.SemaphoreType.DMA((3,)),
            pltpu.SemaphoreType.REGULAR((3, 2)),
        ]
        vm = pl.BlockSpec(memory_space=pltpu.VMEM)
        hbm = pl.BlockSpec(memory_space=pl.ANY)
        return pl.pallas_call(
            functools.partial(moe_kernel, widths, fdim, f_tile),
            out_shape=jax.ShapeDtypeStruct((tok, hid), BF16),
            in_specs=[vm, vm, hbm, hbm, hbm],
            out_specs=vm,
            scratch_shapes=scratch,
            compiler_params=pltpu.CompilerParams(collective_id=0, has_side_effects=True, vmem_limit_bytes=67043328),
            name='moe',
        )(x4, meta, w_g[0], w_u[0], w_d[0])

    tok_spec = P(TOKEN_AXES, None)
    w_spec = P(EXPERT_AXES, None, None)
    return jax.shard_map(local_layer, mesh=mesh, in_specs=(tok_spec, tok_spec, tok_spec, w_spec, w_spec, w_spec), out_specs=tok_spec, check_vma=False)
```

time: 358 us -> 195 us (0.54)
  Pallas kernels: 0 us -> 191 us
  blocking collectives: 121 us -> 0 us
  waiting for transfers between devices: 112 us -> 0 us
  local copies, waits for them, and re-layouts: 52.4 us -> 1.88 us
  matrix products: 43.5 us -> 0 us
  other arithmetic: 17.4 us -> 1.97 us
  starting transfers between devices: 10.8 us -> 0 us
    pallas_call x0 -> x1, Pallas kernels: none -> 191 us  [local_layer(): pl.pallas_call(functools.partial(moe_kernel, widths, fdim, f_tile), out_s...]
    all_to_all x1 -> x0, blocking collectives: 121 us -> none  [local_layer(): recv_buf = lax.all_to_all(send_buf, EXPERT_AXES, 0, 0)]
    all_to_all x1 -> x0, waiting for transfers between devices: 112 us -> none  [local_layer(): back_buf = lax.all_to_all(exp_out, EXPERT_AXES, 0, 0)]
    dot_general x2 -> x0, matrix products: 43.5 us -> none  [the longest x1 25.9 us: local_layer(): jnp.einsum('slcf,lfh->slch', act_bf, w_d, preferred_element_type=jnp.floa...]
    gather x2 -> x0, local copies, waits for them, and re-layouts: 30.9 us -> none  [the longest x1 17.4 us: local_layer(): jnp.take(x_loc, slot_tok, axis=0).reshape(n_dev, n_local, cap_slot, hid_dim)]
    convert_element_type x1 -> x0, local copies, waits for them, and re-layouts: 11.2 us -> none  [local_layer(): jnp.einsum('slcf,lfh->slch', act_bf, w_d, preferred_element_type=jnp.floa...]
    all_to_all x1 -> x0, starting transfers between devices: 10.8 us -> none  [local_layer(): back_buf = lax.all_to_all(exp_out, EXPERT_AXES, 0, 0)]
    select_n x3 -> x0, other arithmetic: 7.45 us -> none  [the longest x1 7.44 us: local_layer(): jnp.take(x_loc, slot_tok, axis=0).reshape(n_dev, n_local, cap_slot, hid_dim)]
  transfers between devices with their start and end apart: 1 -> 0, of which waited for: 1 -> 0; matrix products, arithmetic and copies ran while one was open for 0% -> 0% of each run, Pallas kernels for 0% -> 0%
where the time goes in v1:
time: 195 us
  Pallas kernels  191 us (98%)
  other arithmetic  1.97 us (1%)
    pallas_call x1, Pallas kernels, local_layer(): pl.pallas_call(functools.partial(moe_kernel, widths, fdim, f_tile), out_s...  191 us

profile of v1, /device:TPU:1, one launch (start us, length us, event | category | flops | bytes accessed | tf_op | source)
XLA Modules:
  0.0 194.5 jit_solution(12974020256858235463)
XLA Ops:
  0.0 0.7 convert_bitcast_fusion
  0.7 1.3 pad_maximum_fusion.meta_ref
  2.0 190.7 %moe.1 = bf16[128,2048]{1,0:T(8,128)(2,1)} custom-call(bf16[2,4,16,2048]{3,2,1,0:T(8,128)(2,1)} %bitcast.10, f32[16,128]{1,0:T(8,128)} %pad_maximum_fusion.meta_ref, bf16[2048,768]{1,0:T(8,128)(2,1)} %bitcast.7, bf16[2048,768]{1,0:T(8,128)(2,1)} %bitcast.8, bf16[768,2048]{1,0:T(8,128)(2,1)} %bitcast.9), custom_call_target="tpu_custom_call" | custom-call | tf_op jit(solution)/shard_map/moe/pallas_call | solution.py:463
  192.7 1.9 copy.8

commit v2 on v0

v2 whole, which is shorter than its diff:
```python
import functools

import jax
import jax.numpy as jnp
from jax import lax
from jax.experimental import pallas as pl
from jax.experimental.pallas import tpu as pltpu
from jax.sharding import PartitionSpec as P

TOKEN_AXES = ('ez', 'ey', 'ex')
EXPERT_AXES = ('ex', 'ey', 'ez')
MESH = pl.DeviceIdType.MESH
F32 = jnp.float32
BF16 = jnp.bfloat16

Z, Y, X = 0, 1, 2
D1 = (Y, Z, X)
D2 = (Z, X, Y)
D3 = (X, Y, Z)
A_IS_D1 = (True, False, True)
RING = 4
CORES = 2
CAP = 16
TOK = 128
LEAD = (CORES, RING, RING, RING)


NQ = 6
W1, W2 = (0, 1, 2), (3, 4, 5)


def split_width(hid):
    tiles = hid // 128
    return tuple((tiles * (i + 1) // NQ - tiles * i // NQ) * 128 for i in ORDER)


ORDER = (1, 2, 4, 5, 0, 3)


def moe_kernel(widths, fdim, f_tile, x_ref, meta_ref, w1_hbm, w3_hbm, w2_hbm, y_ref, *scr):
    it = iter(scr)
    take = lambda n: [next(it) for _ in range(n)]
    gat, til, rec = take(NQ), take(NQ), take(NQ)
    meta, sel, comb = take(3), take(3), take(3)
    pas3, pas4, pas5 = take(NQ), take(NQ), take(NQ)
    part, prec, pas6 = take(NQ), take(NQ), take(NQ)
    w1, w3, w2, act = take(4)
    send_sem, recv_sem, w_sem, credit = take(4)

    offs = [sum(widths[:q]) for q in range(NQ)]
    ez, ey, ex = lax.axis_index('ez'), lax.axis_index('ey'), lax.axis_index('ex')
    core = lax.rem(ex, CORES)
    pos = (ez, ey, ex // CORES)
    mod = lambda v: lax.rem(v + RING, RING)
    other = 1 - core

    def peer(dim, off, c):
        q = [mod(pos[d] + off) if d == dim else pos[d] for d in range(3)]
        return (q[0], q[1], q[2] * CORES + c)

    counter = [0]

    def send(src, dst, dev):
        i = counter[0]
        counter[0] += 1
        cp = pltpu.make_async_remote_copy(src, dst, send_sem.at[i], recv_sem.at[i], device_id=dev, device_id_type=MESH)
        cp.start()
        return cp

    bar = pltpu.get_barrier_semaphore()
    npeer = 0
    for dim in range(3):
        for off in (1, -1):
            for c in (core, other):
                pl.semaphore_signal(bar, inc=1, device_id=peer(dim, off, c), device_id_type=MESH)
                npeer += 1
    pl.semaphore_signal(bar, inc=1, device_id=peer(0, 0, other), device_id_type=MESH)
    w_copies = [pltpu.make_async_copy(s, d, w_sem.at[i]) for i, (s, d) in enumerate(((w1_hbm, w1), (w3_hbm, w3), (w2_hbm, w2)))]
    pl.semaphore_wait(bar, npeer + 1)

    DIRS = (1, -1)
    d1 = [D1[q % 3] for q in range(NQ)]
    d2 = [D2[q % 3] for q in range(NQ)]
    d3 = [D3[q % 3] for q in range(NQ)]
    a1 = [A_IS_D1[q % 3] for q in range(NQ)]
    p1 = [pos[d] for d in d1]
    p2 = [pos[d] for d in d2]
    p3 = [pos[d] for d in d3]
    xcol = [x_ref.at[:, :, :, pl.ds(offs[q], widths[q])] for q in range(NQ)]
    unwaited = []

    def chunk(q, r):
        return gat[q].at[:, :, p2[q], mod(p1[q] + r)]

    m1 = [[None, None] for _ in range(3)]
    mf1 = [None] * 3
    m2 = [[None, None] for _ in range(3)]
    mf2 = [None] * 3
    g1 = [[None, None] for _ in range(NQ)]
    f1 = [[None, None] for _ in range(NQ)]
    g2 = [[[None] * 4, [None] * 4] for _ in range(NQ)]
    f2 = [[None] * 4 for _ in range(NQ)]

    def first_sends(wave):
        for q in wave:
            for i, d in enumerate(DIRS):
                if q < 3:
                    m1[q][i] = send(meta_ref, meta[q].at[p2[q], p1[q]], peer(d1[q], d, core))
                g1[q][i] = send(xcol[q], chunk(q, 0), peer(d1[q], d, core))
        for q in wave:
            for i, d in enumerate(DIRS):
                g2[q][i][0] = send(xcol[q], chunk(q, 0), peer(d2[q], d, core))

    def first_forwards(wave):
        for q in wave:
            for i, d in enumerate(DIRS):
                if q < 3:
                    m1[q][i].wait_recv()
                    if i == 0:
                        src = meta[q].at[p2[q], mod(p1[q] - 1)]
                        mf1[q] = send(src, src, peer(d1[q], 1, core))
                g1[q][i].wait_recv()
                half = chunk(q, -d).at[i]
                f1[q][i] = send(half, half, peer(d1[q], d, core))
        for q in wave:
            for i, d in enumerate(DIRS):
                for r in (1, 3):
                    g2[q][i][r] = send(chunk(q, r), chunk(q, r), peer(d2[q], d, core))

    def forward2(q, i, r):
        g2[q][i][r].wait_recv()
        src = gat[q].at[:, :, mod(p2[q] - DIRS[i]), mod(p1[q] + r)]
        f2[q][r] = send(src, src, peer(d2[q], DIRS[i], core))

    first_sends(W1)
    first_sends(W2)
    for c in w_copies:
        c.start()
    for q in range(NQ):
        gat[q][:, :, p2[q], p1[q]] = x_ref[:, :, :, offs[q]:offs[q] + widths[q]]
    for k in range(3):
        meta[k][p2[k], p1[k]] = meta_ref[...]
    first_forwards(W1)
    for k in range(3):
        mf1[k].wait_recv()
        for i, d in enumerate(DIRS):
            row = meta[k].at[p2[k]]
            m2[k][i] = send(row, row, peer(d2[k], d, core))
    first_forwards(W2)
    for q in W1 + W2:
        forward2(q, 0, 0)
        for i, d in enumerate(DIRS):
            f1[q][i].wait_recv()
        for i, d in enumerate(DIRS):
            g2[q][i][2] = send(chunk(q, 2), chunk(q, 2), peer(d2[q], d, core))
    for k in range(3):
        for i in range(2):
            m2[k][i].wait_recv()
        src = meta[k].at[mod(p2[k] - 1)]
        mf2[k] = send(src, src, peer(d2[k], 1, core))

    tri = (lax.broadcasted_iota(jnp.int32, (TOK, TOK), 0) < lax.broadcasted_iota(jnp.int32, (TOK, TOK), 1)).astype(BF16)
    i8 = lax.broadcasted_iota(jnp.int32, (8, 1), 0)
    stride3 = (2 * RING * RING, RING, 1)
    strides = (1, RING, 2 * RING * RING)
    slot = lax.broadcasted_iota(jnp.int32, (8, CAP, TOK), 1).astype(F32)

    def experts8(k):
        base = pos[D1[k]] * strides[D1[k]] + pos[D2[k]] * strides[D2[k]]
        return (base + (i8 & 3) * stride3[k] + (i8 >> 2) * (RING * RING)).astype(F32)

    def picked(ids, evec):
        m = (ids[0:1, :] == evec).astype(F32)
        for j in range(1, 8):
            m = m + (ids[j:j + 1, :] == evec).astype(F32)
        return m

    def rank_of(m):
        rank = jnp.dot(m.astype(BF16), tri, preferred_element_type=F32)
        return jnp.where(m > 0.5, rank, -1.0)

    def onehot(k, i):
        evec = experts8(k)
        rm = rank_of(jnp.concatenate([picked(meta[k][i, j, 0:8], evec) for j in range(4)], axis=0))
        for j in range(4):
            hot = (rm[j * 8:(j + 1) * 8][:, None, :] == slot).astype(F32)
            sel[k][i, j] = hot.reshape(TOK, TOK).astype(BF16)

    def select(q, i):
        k, w = q % 3, widths[q]
        for j in range(4):
            rows = gat[q][:, :, i, j].reshape(TOK, w)
            out = jnp.dot(sel[k][i, j], rows, preferred_element_type=F32).astype(BF16).reshape(CORES, RING, CAP, w)
            if a1[q]:
                til[q][:, :, j, i] = out
            else:
                til[q][:, :, i, j] = out

    def loop(n, f):
        def body(i, carry):
            f(i)
            return carry
        lax.fori_loop(0, n, body, 0)

    for k in range(3):
        onehot(k, p2[k])
    for q in W1 + W2:
        select(q, p2[q])
    for q in W1:
        forward2(q, 0, 1)
        forward2(q, 1, 3)
    for k in range(3):
        mf2[k].wait_recv()
        loop(3, lambda i, k=k: onehot(k, mod(p2[k] + 1 + i)))
    for q in W2:
        forward2(q, 0, 1)
        forward2(q, 1, 3)
    for q in W1 + W2:
        forward2(q, 1, 2)

    def gathered(q, near):
        if near:
            for i, r in ((0, 2), (0, 3), (1, 0), (1, 1)):
                g2[q][i][r].wait_recv()
            loop(2, lambda i, q=q: select(q, mod(p2[q] - 1 + 2 * i)))
        else:
            for r in range(4):
                f2[q][r].wait_recv()
            select(q, mod(p2[q] + 2))
            done = g1[q] + f1[q] + g2[q][0] + g2[q][1] + f2[q]
            if q < 3:
                done = done + m1[q] + [mf1[q]] + m2[q] + [mf2[q]]
            for c in done:
                c.wait_send()

    def sub(ref, q, c, d, half=None):
        a = slice(None) if half is None else pl.ds(2 * half, 2)
        return (ref.at[c, d, a], ref.at[c, a, d], ref.at[c, a, :, d])[q % 3]

    def til_block(ref, q, c, d, half=None):
        return ref.at[c, d] if half is None else ref.at[c, d, pl.ds(2 * half, 2)]

    class Leg:
        def __init__(self, q, cr, src, src_block, dst, dst_block, pas):
            self.a = (q, cr, src, src_block, dst, dst_block, pas)
            self.c = core if cr == 0 else other
            self.first, self.direct = [], []

        def far(self):
            q, cr, src, src_block, dst, dst_block, pas = self.a
            for i, d in enumerate(DIRS):
                self.first.append(send(src_block(src, q, self.c, mod(p3[q] + 2), i), pas.at[i, cr], peer(d3[q], d, core)))

        def near(self):
            q, cr, src, src_block, dst, dst_block, pas = self.a
            for i, d in enumerate(DIRS):
                self.direct.append(send(src_block(src, q, self.c, mod(p3[q] + d)), dst_block(dst, q, core, p3[q]), peer(d3[q], d, self.c)))
            if cr == 1:
                self.direct.append(send(src_block(src, q, self.c, p3[q]), dst_block(dst, q, core, p3[q]), peer(d3[q], 0, other)))

        def forward(self):
            q, cr, src, src_block, dst, dst_block, pas = self.a
            for i, d in enumerate(DIRS):
                self.first[i].wait_recv()
                self.direct.append(send(pas.at[i, cr], dst_block(dst, q, core, mod(p3[q] - d), i), peer(d3[q], d, self.c)))

        def arrive(self):
            for cp in self.direct:
                cp.wait_recv()

        def sent(self):
            for cp in self.first + self.direct:
                cp.wait_send()

    def keep3(q):
        v = til[q][core, p3[q]]
        if q % 3 == 0:
            rec[q][core, p3[q]] = v
        elif q % 3 == 1:
            rec[q][core, :, p3[q]] = v
        else:
            rec[q][core, :, :, p3[q]] = v

    def keep4(q):
        if q % 3 == 0:
            v = til[q][core, p3[q]]
        elif q % 3 == 1:
            v = til[q][core, :, p3[q]]
        else:
            v = til[q][core, :, :, p3[q]]
        gat[q][core, p3[q]] = v

    x3 = [[Leg(q, cr, til[q], til_block, rec[q], sub, pas3[q]) for cr in range(2)] for q in range(NQ)]
    for q in W1:
        gathered(q, True)
    for q in W1:
        gathered(q, False)
        for cr in range(2):
            x3[q][cr].far()
        for cr in range(2):
            x3[q][cr].near()
    for q in W2:
        gathered(q, True)
    for q in W2:
        gathered(q, False)
        for cr in range(2):
            x3[q][cr].far()
    for q in W1:
        for cr in range(2):
            x3[q][cr].forward()
    for q in W2:
        for cr in range(2):
            x3[q][cr].near()
    for q in W1 + W2:
        keep3(q)
    for q in W2:
        for cr in range(2):
            x3[q][cr].forward()
    for c in w_copies:
        c.wait()
    for q in range(NQ):
        for cr in range(2):
            x3[q][cr].arrive()
    for q in range(NQ):
        for cr in range(2):
            x3[q][cr].sent()

    x4 = [[Leg(q, cr, til[q], sub, gat[q], til_block, pas4[q]) for cr in range(2)] for q in range(NQ)]
    rows = 2 * RING * RING * CAP
    for cr in range(2):
        c = core if cr == 0 else other

        def hidden(i, c=c):
            xs = [rec[q][c, pl.ds(2 * i, 2)].reshape(rows, widths[q]) for q in range(NQ)]
            for f in range(fdim // f_tile):
                cols = slice(f * f_tile, (f + 1) * f_tile)
                hg = sum(jnp.dot(xs[q], w1[offs[q]:offs[q] + widths[q], cols], preferred_element_type=F32) for q in range(NQ))
                hu = sum(jnp.dot(xs[q], w3[offs[q]:offs[q] + widths[q], cols], preferred_element_type=F32) for q in range(NQ))
                act[i, :, cols] = (hg * jax.nn.sigmoid(hg) * hu).astype(BF16)

        def down(wave, c=c):
            def step(i):
                for q in wave:
                    o = jnp.dot(act[i], w2[:, offs[q]:offs[q] + widths[q]], preferred_element_type=F32).astype(BF16)
                    til[q][c, pl.ds(2 * i, 2)] = o.reshape(2, RING, RING, CAP, widths[q])
            loop(2, step)

        loop(2, hidden)
        down(W1)
        if cr == 1:
            for q in W1 + W2:
                x4[q][0].forward()
        for q in W1:
            x4[q][cr].far()
        for q in W1:
            x4[q][cr].near()
        down(W2)
        for q in W2:
            x4[q][cr].far()
        if cr == 1:
            for q in W1:
                x4[q][1].forward()
        for q in W2:
            x4[q][cr].near()
        if cr == 0:
            for q in W1 + W2:
                keep4(q)
    for k in range(3):
        for i, d in enumerate(DIRS):
            pl.semaphore_signal(credit.at[k, i], inc=1, device_id=peer(D1[k], d, core), device_id_type=MESH)

    def weights(k, i):
        mrow = meta[k][i, p1[k]]
        ids, gates = mrow[0:8], mrow[8:16]
        own = pos[D2[k]] * strides[D2[k]]
        ms, gs = [], []
        for b in range(4):
            idx = i8 + b * 8
            d3e, d1e, ce = idx & 3, (idx >> 2) & 3, idx >> 4
            evec = (own + d3e * stride3[k] + d1e * strides[D1[k]] + ce * (RING * RING)).astype(F32)
            m = jnp.zeros((8, TOK), F32)
            g = jnp.zeros((8, TOK), F32)
            for j in range(8):
                hit = ids[j:j + 1, :] == evec
                m = m + hit.astype(F32)
                g = g + jnp.where(hit, gates[j:j + 1, :], 0.0)
            ms.append(m)
            gs.append(g)
        rm = rank_of(jnp.concatenate(ms, axis=0))
        for b in range(4):
            hot = jnp.where(rm[b * 8:(b + 1) * 8][:, None, :] == slot, gs[b][:, None, :], 0.0).reshape(TOK, TOK).T
            hi = hot.astype(BF16)
            r1 = hot - hi.astype(F32)
            mid = r1.astype(BF16)
            lo = (r1 - mid.astype(F32)).astype(BF16)
            comb[k][i, b, 0] = hi
            comb[k][i, b, 1] = mid
            comb[k][i, b, 2] = lo

    for q in W2:
        x4[q][1].forward()
    for k in range(3):
        loop(4, lambda i, k=k: weights(k, i))

    def from_src(ref, q, d, half=None):
        cs = slice(None) if half is None else half
        return ref.at[cs, :, d] if a1[q] else ref.at[cs, :, :, d]

    x5 = [([], []) for _ in range(NQ)]

    def arrive4(q):
        for cr in range(2):
            x4[q][cr].arrive()
        if q < 3:
            for i in range(2):
                pl.semaphore_wait(credit.at[q, i], 1)

    def far5(q):
        for i, d in enumerate(DIRS):
            x5[q][0].append(send(from_src(gat[q], q, mod(p1[q] + 2), i), pas5[q].at[i], peer(d1[q], d, core)))

    def near5(q):
        for i, d in enumerate(DIRS):
            x5[q][1].append(send(from_src(gat[q], q, mod(p1[q] + d)), rec[q].at[:, p1[q]], peer(d1[q], d, core)))

    def keep5(q):
        if a1[q]:
            rec[q][:, p1[q]] = gat[q][:, :, p1[q]]
        else:
            rec[q][:, p1[q]] = gat[q][:, :, :, p1[q]]

    def forward5(q):
        for i, d in enumerate(DIRS):
            x5[q][0][i].wait_recv()
            x5[q][1].append(send(pas5[q].at[i], rec[q].at[i, mod(p1[q] - d)], peer(d1[q], d, core)))

    for q in W1:
        arrive4(q)
        far5(q)
        near5(q)
    for q in W1:
        keep5(q)
    for q in W2:
        arrive4(q)
        far5(q)
    for q in W1:
        forward5(q)
    for q in W2:
        near5(q)
    for q in W2:
        keep5(q)
    for q in W2:
        forward5(q)

    x6 = [([], []) for _ in range(NQ)]
    half_tok = TOK // 2

    def combine(q):
        for cp in x5[q][1]:
            cp.wait_recv()
        k, w = q % 3, widths[q]

        def step(i):
            acc = jnp.zeros((TOK, w), F32)
            for b in range(4):
                o = rec[q][b // 2, pl.ds(2 * (b % 2), 2), :, i].reshape(TOK, w)
                for t in range(3):
                    acc = acc + jnp.dot(comb[k][i, b, t], o, preferred_element_type=F32)
            part[q][i] = acc

        loop(4, step)

    def far6(q):
        for i, d in enumerate(DIRS):
            x6[q][0].append(send(part[q].at[mod(p2[q] + 2), pl.ds(i * half_tok, half_tok)], pas6[q].at[i], peer(d2[q], d, core)))

    def near6(q):
        for i, d in enumerate(DIRS):
            x6[q][1].append(send(part[q].at[mod(p2[q] + d)], prec[q].at[i], peer(d2[q], d, core)))

    def forward6(q):
        for i, d in enumerate(DIRS):
            x6[q][0][i].wait_recv()
            x6[q][1].append(send(pas6[q].at[i], prec[q].at[2, pl.ds(i * half_tok, half_tok)], peer(d2[q], d, core)))

    def final(q):
        for cp in x6[q][1]:
            cp.wait_recv()
        total = part[q][p2[q]] + prec[q][0] + prec[q][1] + prec[q][2]
        xk = x_ref[:, :, :, offs[q]:offs[q] + widths[q]].reshape(TOK, widths[q]).astype(F32)
        y_ref[:, offs[q]:offs[q] + widths[q]] = (xk + total).astype(BF16)

    for q in W1:
        combine(q)
        far6(q)
        near6(q)
    for q in W2:
        combine(q)
        far6(q)
    for q in W1:
        forward6(q)
    for q in W2:
        near6(q)
    for q in W2:
        forward6(q)
    for q in W1 + W2:
        final(q)
    for q in range(NQ):
        for cr in range(2):
            x4[q][cr].sent()
        for cp in x5[q][0] + x5[q][1] + x6[q][0] + x6[q][1]:
            cp.wait_send()


N_COPIES = 3 * 7 + NQ * (16 + 14 + 14 + 6 + 6)


def solution(mesh):
    def local_layer(x_loc, ids_loc, gates_loc, w_g, w_u, w_d):
        tok, hid = x_loc.shape
        fdim = w_g.shape[2]
        widths = split_width(hid)
        f_tile = 256 if fdim % 256 == 0 else fdim
        meta = jnp.concatenate([ids_loc.T.astype(F32), gates_loc.T], axis=0)
        x4 = x_loc.reshape(CORES, RING, CAP, hid)
        scratch = []
        each = lambda f: scratch.extend(f(w) for w in widths)
        for _ in range(3):
            each(lambda w: pltpu.VMEM(LEAD + (CAP, w), BF16))
        scratch += [pltpu.VMEM((RING, RING, 16, TOK), F32)] * 3
        scratch += [pltpu.VMEM((RING, RING, TOK, TOK), BF16)] * 3
        scratch += [pltpu.VMEM((RING, 4, 3, TOK, TOK), BF16)] * 3
        each(lambda w: pltpu.VMEM((2, CORES, 2, RING, CAP, w), BF16))
        each(lambda w: pltpu.VMEM((2, CORES, 2, RING, CAP, w), BF16))
        each(lambda w: pltpu.VMEM((2, RING, RING, CAP, w), BF16))
        each(lambda w: pltpu.VMEM((RING, TOK, w), F32))
        each(lambda w: pltpu.VMEM((3, TOK, w), F32))
        each(lambda w: pltpu.VMEM((2, TOK // 2, w), F32))
        scratch += [
            pltpu.VMEM((hid, fdim), BF16),
            pltpu.VMEM((hid, fdim), BF16),
            pltpu.VMEM((fdim, hid), BF16),
            pltpu.VMEM((2, 2 * RING * RING * CAP, fdim), BF16),
            pltpu.SemaphoreType.DMA((N_COPIES,)),
            pltpu.SemaphoreType.DMA((N_COPIES,)),
            pltpu.SemaphoreType.DMA((3,)),
            pltpu.SemaphoreType.REGULAR((3, 2)),
        ]
        vm = pl.BlockSpec(memory_space=pltpu.VMEM)
        hbm = pl.BlockSpec(memory_space=pl.ANY)
        return pl.pallas_call(
            functools.partial(moe_kernel, widths, fdim, f_tile),
            out_shape=jax.ShapeDtypeStruct((tok, hid), BF16),
            in_specs=[vm, vm, hbm, hbm, hbm],
            out_specs=vm,
            scratch_shapes=scratch,
            compiler_params=pltpu.CompilerParams(collective_id=0, has_side_effects=True, vmem_limit_bytes=67043328),
            name='moe',
        )(x4, meta, w_g[0], w_u[0], w_d[0])

    tok_spec = P(TOKEN_AXES, None)
    w_spec = P(EXPERT_AXES, None, None)
    return jax.shard_map(local_layer, mesh=mesh, in_specs=(tok_spec, tok_spec, tok_spec, w_spec, w_spec, w_spec), out_specs=tok_spec, check_vma=False)
```

time: 358 us -> 188 us (0.53)
  Pallas kernels: 0 us -> 184 us
  blocking collectives: 121 us -> 0 us
  waiting for transfers between devices: 112 us -> 0 us
  local copies, waits for them, and re-layouts: 52.4 us -> 1.88 us
  matrix products: 43.5 us -> 0 us
  other arithmetic: 17.4 us -> 1.97 us
  starting transfers between devices: 10.8 us -> 0 us
    pallas_call x0 -> x1, Pallas kernels: none -> 184 us  [local_layer(): pl.pallas_call(functools.partial(moe_kernel, widths, fdim, f_tile), out_s...]
    all_to_all x1 -> x0, blocking collectives: 121 us -> none  [local_layer(): recv_buf = lax.all_to_all(send_buf, EXPERT_AXES, 0, 0)]
    all_to_all x1 -> x0, waiting for transfers between devices: 112 us -> none  [local_layer(): back_buf = lax.all_to_all(exp_out, EXPERT_AXES, 0, 0)]
    dot_general x2 -> x0, matrix products: 43.5 us -> none  [the longest x1 25.9 us: local_layer(): jnp.einsum('slcf,lfh->slch', act_bf, w_d, preferred_element_type=jnp.floa...]
    gather x2 -> x0, local copies, waits for them, and re-layouts: 30.9 us -> none  [the longest x1 17.4 us: local_layer(): jnp.take(x_loc, slot_tok, axis=0).reshape(n_dev, n_local, cap_slot, hid_dim)]
    convert_element_type x1 -> x0, local copies, waits for them, and re-layouts: 11.2 us -> none  [local_layer(): jnp.einsum('slcf,lfh->slch', act_bf, w_d, preferred_element_type=jnp.floa...]
    all_to_all x1 -> x0, starting transfers between devices: 10.8 us -> none  [local_layer(): back_buf = lax.all_to_all(exp_out, EXPERT_AXES, 0, 0)]
    select_n x3 -> x0, other arithmetic: 7.45 us -> none  [the longest x1 7.44 us: local_layer(): jnp.take(x_loc, slot_tok, axis=0).reshape(n_dev, n_local, cap_slot, hid_dim)]
  transfers between devices with their start and end apart: 1 -> 0, of which waited for: 1 -> 0; matrix products, arithmetic and copies ran while one was open for 0% -> 0% of each run, Pallas kernels for 0% -> 0%
where the time goes in v2:
time: 188 us
  Pallas kernels  184 us (98%)
  other arithmetic  1.97 us (1%)
    pallas_call x1, Pallas kernels, local_layer(): pl.pallas_call(functools.partial(moe_kernel, widths, fdim, f_tile), out_s...  184 us

profile of v2, /device:TPU:1, one launch (start us, length us, event | category | flops | bytes accessed | tf_op | source)
XLA Modules:
  0.0 187.8 jit_solution(1761717385100015809)
XLA Ops:
  0.0 0.7 convert_bitcast_fusion
  0.7 1.3 pad_maximum_fusion.meta_ref
  2.0 183.9 %moe.1 = bf16[128,2048]{1,0:T(8,128)(2,1)} custom-call(bf16[2,4,16,2048]{3,2,1,0:T(8,128)(2,1)} %bitcast.10, f32[16,128]{1,0:T(8,128)} %pad_maximum_fusion.meta_ref, bf16[2048,768]{1,0:T(8,128)(2,1)} %bitcast.7, bf16[2048,768]{1,0:T(8,128)(2,1)} %bitcast.8, bf16[768,2048]{1,0:T(8,128)(2,1)} %bitcast.9), custom_call_target="tpu_custom_call" | custom-call | tf_op jit(solution)/shard_map/moe/pallas_call | solution.py:551
  185.9 1.9 %copy.8 = bf16[128,2048]{1,0:T(8,128)(2,1)} copy(bf16[128,2048]{1,0:T(8,128)(2,1)} %moe.1) | data formatting | bytes 1048576

commit v3 on v2

--- a/solution.py
+++ b/solution.py
@@ -295,40 +295,39 @@
         gathered(q, True)
     for q in W1:
         gathered(q, False)
-        for cr in range(2):
-            x3[q][cr].far()
-        for cr in range(2):
-            x3[q][cr].near()
+        x3[q][0].far()
+        x3[q][0].near()
     for q in W2:
         gathered(q, True)
     for q in W2:
         gathered(q, False)
-        for cr in range(2):
-            x3[q][cr].far()
-    for q in W1:
-        for cr in range(2):
-            x3[q][cr].forward()
-    for q in W2:
-        for cr in range(2):
-            x3[q][cr].near()
+        x3[q][0].far()
+    for q in W1:
+        x3[q][1].far()
+    for q in W1:
+        x3[q][0].forward()
+    for q in W2:
+        x3[q][0].near()
+        x3[q][1].far()
+    for q in W2:
+        x3[q][0].forward()
+    for q in W1 + W2:
+        x3[q][1].near()
     for q in W1 + W2:
         keep3(q)
-    for q in W2:
-        for cr in range(2):
-            x3[q][cr].forward()
+    for q in W1 + W2:
+        x3[q][1].forward()
     for c in w_copies:
         c.wait()
-    for q in range(NQ):
-        for cr in range(2):
-            x3[q][cr].arrive()
-    for q in range(NQ):
-        for cr in range(2):
-            x3[q][cr].sent()
 
     x4 = [[Leg(q, cr, til[q], sub, gat[q], til_block, pas4[q]) for cr in range(2)] for q in range(NQ)]
     rows = 2 * RING * RING * CAP
     for cr in range(2):
         c = core if cr == 0 else other
+        for q in range(NQ):
+            x3[q][cr].arrive()
+        for q in range(NQ):
+            x3[q][cr].sent()
 
         def hidden(i, c=c):
             xs = [rec[q][c, pl.ds(2 * i, 2)].reshape(rows, widths[q]) for q in range(NQ)]
@@ -474,19 +473,24 @@
         for i, d in enumerate(DIRS):
             x6[q][0].append(send(part[q].at[mod(p2[q] + 2), pl.ds(i * half_tok, half_tok)], pas6[q].at[i], peer(d2[q], d, core)))
 
+    def rows6(q, i, half):
+        return part[q].at[mod(p2[q] + DIRS[i]), pl.ds(half * half_tok, half_tok)], prec[q].at[i, pl.ds(half * half_tok, half_tok)]
+
     def near6(q):
         for i, d in enumerate(DIRS):
-            x6[q][1].append(send(part[q].at[mod(p2[q] + d)], prec[q].at[i], peer(d2[q], d, core)))
+            x6[q][1].append(send(*rows6(q, i, 1 - i), peer(d2[q], d, core)))
 
     def forward6(q):
         for i, d in enumerate(DIRS):
             x6[q][0][i].wait_recv()
-            x6[q][1].append(send(pas6[q].at[i], prec[q].at[2, pl.ds(i * half_tok, half_tok)], peer(d2[q], d, core)))
+            mine, there = rows6(q, i, i)
+            mine[...] = mine[...] + pas6[q][i]
+            x6[q][1].append(send(mine, there, peer(d2[q], d, core)))
 
     def final(q):
         for cp in x6[q][1]:
             cp.wait_recv()
-        total = part[q][p2[q]] + prec[q][0] + prec[q][1] + prec[q][2]
+        total = part[q][p2[q]] + prec[q][0] + prec[q][1]
         xk = x_ref[:, :, :, offs[q]:offs[q] + widths[q]].reshape(TOK, widths[q]).astype(F32)
         y_ref[:, offs[q]:offs[q] + widths[q]] = (xk + total).astype(BF16)
 
@@ -512,7 +516,7 @@
             cp.wait_send()
 
 
-N_COPIES = 3 * 7 + NQ * (16 + 14 + 14 + 6 + 6)
+N_COPIES = 3 * 6 + NQ * (16 + 13 + 13 + 6 + 6)
 
 
 def solution(mesh):
@@ -534,7 +538,7 @@
         each(lambda w: pltpu.VMEM((2, CORES, 2, RING, CAP, w), BF16))
         each(lambda w: pltpu.VMEM((2, RING, RING, CAP, w), BF16))
         each(lambda w: pltpu.VMEM((RING, TOK, w), F32))
-        each(lambda w: pltpu.VMEM((3, TOK, w), F32))
+        each(lambda w: pltpu.VMEM((2, TOK, w), F32))
         each(lambda w: pltpu.VMEM((2, TOK // 2, w), F32))
         scratch += [
             pltpu.VMEM((hid, fdim), BF16),

time: 188 us -> 176 us (0.936); the launches traced: 188 us -> 173 us
  Pallas kernels: 184 us -> 169 us
    pallas_call x1, Pallas kernels: 184 us -> 169 us  [local_layer(): pl.pallas_call(functools.partial(moe_kernel, widths, fdim, f_tile), out_s...]
where the time goes in v3:
time: 176 us; the launch traced here: 173 us
  Pallas kernels  169 us (96%)
  other arithmetic  1.97 us (1%)
  local copies, waits for them, and re-layouts  1.88 us (1%)
    pallas_call x1, Pallas kernels, local_layer(): pl.pallas_call(functools.partial(moe_kernel, widths, fdim, f_tile), out_s...  169 us

profile of v3, /device:TPU:1, one launch (start us, length us, event | category | flops | bytes accessed | tf_op | source)
XLA Modules:
  0.0 172.9 jit_solution(13805466718196801206)
XLA Ops:
  0.0 0.7 convert_bitcast_fusion
  0.7 1.3 pad_maximum_fusion.meta_ref
  2.0 169.1 %moe.1 = bf16[128,2048]{1,0:T(8,128)(2,1)} custom-call(bf16[2,4,16,2048]{3,2,1,0:T(8,128)(2,1)} %bitcast.10, f32[16,128]{1,0:T(8,128)} %pad_maximum_fusion.meta_ref, bf16[2048,768]{1,0:T(8,128)(2,1)} %bitcast.7, bf16[2048,768]{1,0:T(8,128)(2,1)} %bitcast.8, bf16[768,2048]{1,0:T(8,128)(2,1)} %bitcast.9), custom_call_target="tpu_custom_call" | custom-call | tf_op jit(solution)/shard_map/moe/pallas_call | solution.py:555
  171.0 1.9 %copy.8 = bf16[128,2048]{1,0:T(8,128)(2,1)} copy(bf16[128,2048]{1,0:T(8,128)(2,1)} %moe.1) | data formatting | bytes 1048576

commit v4 on v3

--- a/solution.py
+++ b/solution.py
@@ -54,8 +54,14 @@
     mod = lambda v: lax.rem(v + RING, RING)
     other = 1 - core
 
-    def peer(dim, off, c):
-        q = [mod(pos[d] + off) if d == dim else pos[d] for d in range(3)]
+    strides = (1, RING, 2 * RING * RING)
+
+    def turned(v, r):
+        return [v[d] * (1 - r) + v[(d + 1) % 3] * r for d in range(3)]
+
+    def peer(dim, off, c, lane=None):
+        r = core if lane is None else lane
+        q = [mod(pos[j] + off * ((1 - r) * int(j == dim) + r * int(j == (dim + 1) % 3))) for j in range(3)]
         return (q[0], q[1], q[2] * CORES + c)
 
     counter = [0]
@@ -72,7 +78,7 @@
     for dim in range(3):
         for off in (1, -1):
             for c in (core, other):
-                pl.semaphore_signal(bar, inc=1, device_id=peer(dim, off, c), device_id_type=MESH)
+                pl.semaphore_signal(bar, inc=1, device_id=peer(dim, off, c, 0), device_id_type=MESH)
                 npeer += 1
     pl.semaphore_signal(bar, inc=1, device_id=peer(0, 0, other), device_id_type=MESH)
     w_copies = [pltpu.make_async_copy(s, d, w_sem.at[i]) for i, (s, d) in enumerate(((w1_hbm, w1), (w3_hbm, w3), (w2_hbm, w2)))]
@@ -83,9 +89,12 @@
     d2 = [D2[q % 3] for q in range(NQ)]
     d3 = [D3[q % 3] for q in range(NQ)]
     a1 = [A_IS_D1[q % 3] for q in range(NQ)]
-    p1 = [pos[d] for d in d1]
-    p2 = [pos[d] for d in d2]
-    p3 = [pos[d] for d in d3]
+    lpos, lstr = turned(pos, core), turned(strides, core)
+    opos = turned(pos, other)
+    p1 = [lpos[d] for d in d1]
+    p2 = [lpos[d] for d in d2]
+    p3 = [lpos[d] for d in d3]
+    p3_other = [opos[d] for d in d3]
     xcol = [x_ref.at[:, :, :, pl.ds(offs[q], widths[q])] for q in range(NQ)]
     unwaited = []
 
@@ -161,13 +170,11 @@
 
     tri = (lax.broadcasted_iota(jnp.int32, (TOK, TOK), 0) < lax.broadcasted_iota(jnp.int32, (TOK, TOK), 1)).astype(BF16)
     i8 = lax.broadcasted_iota(jnp.int32, (8, 1), 0)
-    stride3 = (2 * RING * RING, RING, 1)
-    strides = (1, RING, 2 * RING * RING)
     slot = lax.broadcasted_iota(jnp.int32, (8, CAP, TOK), 1).astype(F32)
 
     def experts8(k):
-        base = pos[D1[k]] * strides[D1[k]] + pos[D2[k]] * strides[D2[k]]
-        return (base + (i8 & 3) * stride3[k] + (i8 >> 2) * (RING * RING)).astype(F32)
+        base = lpos[D1[k]] * lstr[D1[k]] + lpos[D2[k]] * lstr[D2[k]]
+        return (base + (i8 & 3) * lstr[D3[k]] + (i8 >> 2) * (RING * RING)).astype(F32)
 
     def picked(ids, evec):
         m = (ids[0:1, :] == evec).astype(F32)
@@ -241,28 +248,33 @@
         return ref.at[c, d] if half is None else ref.at[c, d, pl.ds(2 * half, 2)]
 
     class Leg:
-        def __init__(self, q, cr, src, src_block, dst, dst_block, pas):
-            self.a = (q, cr, src, src_block, dst, dst_block, pas)
+        def __init__(self, q, cr, lane, src, src_block, dst, dst_block, pas):
+            self.q, self.cr, self.lane, self.src, self.dst = q, cr, lane, src, dst
+            self.src_block, self.dst_block, self.pas = src_block, dst_block, pas
             self.c = core if cr == 0 else other
+            self.p = p3[q] if lane is core else p3_other[q]
             self.first, self.direct = [], []
 
+        def out(self, d, half=None):
+            return self.src_block(self.src, self.q, self.c, d, half)
+
+        def into(self, d, half=None):
+            return self.dst_block(self.dst, self.q, core, d, half)
+
         def far(self):
-            q, cr, src, src_block, dst, dst_block, pas = self.a
-            for i, d in enumerate(DIRS):
-                self.first.append(send(src_block(src, q, self.c, mod(p3[q] + 2), i), pas.at[i, cr], peer(d3[q], d, core)))
+            for i, d in enumerate(DIRS):
+                self.first.append(send(self.out(mod(self.p + 2), i), self.pas.at[i, self.cr], peer(d3[self.q], d, core, self.lane)))
 
         def near(self):
-            q, cr, src, src_block, dst, dst_block, pas = self.a
-            for i, d in enumerate(DIRS):
-                self.direct.append(send(src_block(src, q, self.c, mod(p3[q] + d)), dst_block(dst, q, core, p3[q]), peer(d3[q], d, self.c)))
-            if cr == 1:
-                self.direct.append(send(src_block(src, q, self.c, p3[q]), dst_block(dst, q, core, p3[q]), peer(d3[q], 0, other)))
+            for i, d in enumerate(DIRS):
+                self.direct.append(send(self.out(mod(self.p + d)), self.into(self.p), peer(d3[self.q], d, self.c, self.lane)))
+            if self.cr == 1:
+                self.direct.append(send(self.out(self.p), self.into(self.p), peer(d3[self.q], 0, other, self.lane)))
 
         def forward(self):
-            q, cr, src, src_block, dst, dst_block, pas = self.a
             for i, d in enumerate(DIRS):
                 self.first[i].wait_recv()
-                self.direct.append(send(pas.at[i, cr], dst_block(dst, q, core, mod(p3[q] - d), i), peer(d3[q], d, self.c)))
+                self.direct.append(send(self.pas.at[i, self.cr], self.into(mod(self.p - d), i), peer(d3[self.q], d, self.c, self.lane)))
 
         def arrive(self):
             for cp in self.direct:
@@ -290,7 +302,7 @@
             v = til[q][core, :, :, p3[q]]
         gat[q][core, p3[q]] = v
 
-    x3 = [[Leg(q, cr, til[q], til_block, rec[q], sub, pas3[q]) for cr in range(2)] for q in range(NQ)]
+    x3 = [[Leg(q, cr, core, til[q], til_block, rec[q], sub, pas3[q]) for cr in range(2)] for q in range(NQ)]
     for q in W1:
         gathered(q, True)
     for q in W1:
@@ -320,7 +332,7 @@
     for c in w_copies:
         c.wait()
 
-    x4 = [[Leg(q, cr, til[q], sub, gat[q], til_block, pas4[q]) for cr in range(2)] for q in range(NQ)]
+    x4 = [[Leg(q, cr, core if cr == 0 else other, til[q], sub, gat[q], til_block, pas4[q]) for cr in range(2)] for q in range(NQ)]
     rows = 2 * RING * RING * CAP
     for cr in range(2):
         c = core if cr == 0 else other
@@ -371,12 +383,12 @@
     def weights(k, i):
         mrow = meta[k][i, p1[k]]
         ids, gates = mrow[0:8], mrow[8:16]
-        own = pos[D2[k]] * strides[D2[k]]
+        own = lpos[D2[k]] * lstr[D2[k]]
         ms, gs = [], []
         for b in range(4):
             idx = i8 + b * 8
             d3e, d1e, ce = idx & 3, (idx >> 2) & 3, idx >> 4
-            evec = (own + d3e * stride3[k] + d1e * strides[D1[k]] + ce * (RING * RING)).astype(F32)
+            evec = (own + d3e * lstr[D3[k]] + d1e * lstr[D1[k]] + ce * (RING * RING)).astype(F32)
             m = jnp.zeros((8, TOK), F32)
             g = jnp.zeros((8, TOK), F32)
             for j in range(8):

time: 176 us -> 172 us (0.977); the launches traced: 173 us -> 172 us
  no operation moved by 1% of the time
where the time goes in v4:
time: 172 us
  Pallas kernels  168 us (98%)
  other arithmetic  1.97 us (1%)
  local copies, waits for them, and re-layouts  1.88 us (1%)
    pallas_call x1, Pallas kernels, local_layer(): pl.pallas_call(functools.partial(moe_kernel, widths, fdim, f_tile), out_s...  168 us

profile of v4, /device:TPU:1, one launch (start us, length us, event | category | flops | bytes accessed | tf_op | source)
XLA Modules:
  0.0 172.1 jit_solution(2676884895812429724)
XLA Ops:
  0.0 0.7 convert_bitcast_fusion
  0.7 1.3 pad_maximum_fusion.meta_ref
  2.0 168.3 %moe.1 = bf16[128,2048]{1,0:T(8,128)(2,1)} custom-call(bf16[2,4,16,2048]{3,2,1,0:T(8,128)(2,1)} %bitcast.10, f32[16,128]{1,0:T(8,128)} %pad_maximum_fusion.meta_ref, bf16[2048,768]{1,0:T(8,128)(2,1)} %bitcast.7, bf16[2048,768]{1,0:T(8,128)(2,1)} %bitcast.8, bf16[768,2048]{1,0:T(8,128)(2,1)} %bitcast.9), custom_call_target="tpu_custom_call" | custom-call | tf_op jit(solution)/shard_map/moe/pallas_call | solution.py:567
  170.3 1.9 %copy.8 = bf16[128,2048]{1,0:T(8,128)(2,1)} copy(bf16[128,2048]{1,0:T(8,128)(2,1)} %moe.1) | data formatting | bytes 1048576

commit v5 on v4

--- a/solution.py
+++ b/solution.py
@@ -31,20 +31,20 @@
 
 def split_width(hid):
     tiles = hid // 128
-    return tuple((tiles * (i + 1) // NQ - tiles * i // NQ) * 128 for i in ORDER)
-
-
-ORDER = (1, 2, 4, 5, 0, 3)
-
-
-def moe_kernel(widths, fdim, f_tile, x_ref, meta_ref, w1_hbm, w3_hbm, w2_hbm, y_ref, *scr):
+    second = tiles * 3 // 8
+    first = tiles - second
+    thirds = lambda n: [n - 2 * (n // 3), n // 3, n // 3]
+    return tuple(n * 128 for n in thirds(first) + thirds(second))
+
+
+def moe_kernel(widths, fdim, f_tile, x_ref, ids_ref, gates_ref, w1_hbm, w3_hbm, w2_hbm, y_ref, *scr):
     it = iter(scr)
     take = lambda n: [next(it) for _ in range(n)]
     gat, til, rec = take(NQ), take(NQ), take(NQ)
     meta, sel, comb = take(3), take(3), take(3)
     pas3, pas4, pas5 = take(NQ), take(NQ), take(NQ)
     part, prec, pas6 = take(NQ), take(NQ), take(NQ)
-    w1, w3, w2, act = take(4)
+    w1, w3, w2, act, meta_ref = take(5)
     send_sem, recv_sem, w_sem, credit = take(4)
 
     offs = [sum(widths[:q]) for q in range(NQ)]
@@ -73,6 +73,8 @@
         cp.start()
         return cp
 
+    meta_ref[0:8] = ids_ref[...].astype(F32)
+    meta_ref[8:16] = gates_ref[...]
     bar = pltpu.get_barrier_semaphore()
     npeer = 0
     for dim in range(3):
@@ -342,25 +344,27 @@
             x3[q][cr].sent()
 
         def hidden(i, c=c):
-            xs = [rec[q][c, pl.ds(2 * i, 2)].reshape(rows, widths[q]) for q in range(NQ)]
+            xs = jnp.concatenate([rec[q][c, pl.ds(2 * i, 2)].reshape(rows, widths[q]) for q in range(NQ)], axis=1)
             for f in range(fdim // f_tile):
                 cols = slice(f * f_tile, (f + 1) * f_tile)
-                hg = sum(jnp.dot(xs[q], w1[offs[q]:offs[q] + widths[q], cols], preferred_element_type=F32) for q in range(NQ))
-                hu = sum(jnp.dot(xs[q], w3[offs[q]:offs[q] + widths[q], cols], preferred_element_type=F32) for q in range(NQ))
+                hg = jnp.dot(xs, w1[:, cols], preferred_element_type=F32)
+                hu = jnp.dot(xs, w3[:, cols], preferred_element_type=F32)
                 act[i, :, cols] = (hg * jax.nn.sigmoid(hg) * hu).astype(BF16)
 
         def down(wave, c=c):
             def step(i):
+                lo, hi = offs[wave[0]], offs[wave[-1]] + widths[wave[-1]]
+                o = jnp.dot(act[i], w2[:, lo:hi], preferred_element_type=F32).astype(BF16)
                 for q in wave:
-                    o = jnp.dot(act[i], w2[:, offs[q]:offs[q] + widths[q]], preferred_element_type=F32).astype(BF16)
-                    til[q][c, pl.ds(2 * i, 2)] = o.reshape(2, RING, RING, CAP, widths[q])
+                    part_q = o[:, offs[q] - lo:offs[q] - lo + widths[q]]
+                    til[q][c, pl.ds(2 * i, 2)] = part_q.reshape(2, RING, RING, CAP, widths[q])
             loop(2, step)
 
         loop(2, hidden)
-        down(W1)
         if cr == 1:
             for q in W1 + W2:
                 x4[q][0].forward()
+        down(W1)
         for q in W1:
             x4[q][cr].far()
         for q in W1:
@@ -404,9 +408,10 @@
             r1 = hot - hi.astype(F32)
             mid = r1.astype(BF16)
             lo = (r1 - mid.astype(F32)).astype(BF16)
-            comb[k][i, b, 0] = hi
-            comb[k][i, b, 1] = mid
-            comb[k][i, b, 2] = lo
+            at = slice((b % 2) * TOK, (b % 2 + 1) * TOK)
+            comb[k][i, b // 2, 0, :, at] = hi
+            comb[k][i, b // 2, 1, :, at] = mid
+            comb[k][i, b // 2, 2, :, at] = lo
 
     for q in W2:
         x4[q][1].forward()
@@ -473,10 +478,10 @@
 
         def step(i):
             acc = jnp.zeros((TOK, w), F32)
-            for b in range(4):
-                o = rec[q][b // 2, pl.ds(2 * (b % 2), 2), :, i].reshape(TOK, w)
+            for c in range(2):
+                o = rec[q][c, :, :, i].reshape(2 * TOK, w)
                 for t in range(3):
-                    acc = acc + jnp.dot(comb[k][i, b, t], o, preferred_element_type=F32)
+                    acc = acc + jnp.dot(comb[k][i, c, t], o, preferred_element_type=F32)
             part[q][i] = acc
 
         loop(4, step)
@@ -537,7 +542,6 @@
         fdim = w_g.shape[2]
         widths = split_width(hid)
         f_tile = 256 if fdim % 256 == 0 else fdim
-        meta = jnp.concatenate([ids_loc.T.astype(F32), gates_loc.T], axis=0)
         x4 = x_loc.reshape(CORES, RING, CAP, hid)
         scratch = []
         each = lambda f: scratch.extend(f(w) for w in widths)
@@ -545,7 +549,7 @@
             each(lambda w: pltpu.VMEM(LEAD + (CAP, w), BF16))
         scratch += [pltpu.VMEM((RING, RING, 16, TOK), F32)] * 3
         scratch += [pltpu.VMEM((RING, RING, TOK, TOK), BF16)] * 3
-        scratch += [pltpu.VMEM((RING, 4, 3, TOK, TOK), BF16)] * 3
+        scratch += [pltpu.VMEM((RING, 2, 3, TOK, 2 * TOK), BF16)] * 3
         each(lambda w: pltpu.VMEM((2, CORES, 2, RING, CAP, w), BF16))
         each(lambda w: pltpu.VMEM((2, CORES, 2, RING, CAP, w), BF16))
         each(lambda w: pltpu.VMEM((2, RING, RING, CAP, w), BF16))
@@ -557,6 +561,7 @@
             pltpu.VMEM((hid, fdim), BF16),
             pltpu.VMEM((fdim, hid), BF16),
             pltpu.VMEM((2, 2 * RING * RING * CAP, fdim), BF16),
+            pltpu.VMEM((16, TOK), F32),
             pltpu.SemaphoreType.DMA((N_COPIES,)),
             pltpu.SemaphoreType.DMA((N_COPIES,)),
             pltpu.SemaphoreType.DMA((3,)),
@@ -567,12 +572,12 @@
         return pl.pallas_call(
             functools.partial(moe_kernel, widths, fdim, f_tile),
             out_shape=jax.ShapeDtypeStruct((tok, hid), BF16),
-            in_specs=[vm, vm, hbm, hbm, hbm],
+            in_specs=[vm, vm, vm, hbm, hbm, hbm],
             out_specs=vm,
             scratch_shapes=scratch,
             compiler_params=pltpu.CompilerParams(collective_id=0, has_side_effects=True, vmem_limit_bytes=67043328),
             name='moe',
-        )(x4, meta, w_g[0], w_u[0], w_d[0])
+        )(x4, ids_loc.T, gates_loc.T, w_g[0], w_u[0], w_d[0])
 
     tok_spec = P(TOKEN_AXES, None)
     w_spec = P(EXPERT_AXES, None, None)

time: 172 us -> 164 us (0.953)
  Pallas kernels: 168 us -> 161 us
  other arithmetic: 1.97 us -> 0 us
    pallas_call x1, Pallas kernels: 168 us -> 161 us  [local_layer(): pl.pallas_call(functools.partial(moe_kernel, widths, fdim, f_tile), out_s...]
where the time goes in v5:
time: 164 us; the launch traced here: 163 us
  Pallas kernels  161 us (98%)
  local copies, waits for them, and re-layouts  1.88 us (1%)
    pallas_call x1, Pallas kernels, local_layer(): pl.pallas_call(functools.partial(moe_kernel, widths, fdim, f_tile), out_s...  161 us

profile of v5, /device:TPU:1, one launch (start us, length us, event | category | flops | bytes accessed | tf_op | source)
XLA Modules:
  0.0 163.4 jit_solution(15640063391243923219)
XLA Ops:
  0.0 161.5 %moe.1 = bf16[128,2048]{1,0:T(8,128)(2,1)} custom-call(bf16[2,4,16,2048]{3,2,1,0:T(8,128)(2,1)} %bitcast.9, s32[8,128]{1,0:T(8,128)} %bitcast.10, f32[8,128]{1,0:T(8,128)} %bitcast.11, bf16[2048,768]{1,0:T(8,128)(2,1)} %bitcast.6, bf16[2048,768]{1,0:T(8,128)(2,1)} %bitcast.7, bf16[768,2048]{1,0:T(8,128)(2,1)} %bitcast.8), custom_call_target="tpu_custom_call" | custom-call | tf_op jit(solution)/shard_map/moe/pallas_call | solution.py:572
  161.5 1.9 %copy.8 = bf16[128,2048]{1,0:T(8,128)(2,1)} copy(bf16[128,2048]{1,0:T(8,128)(2,1)} %moe.1) | data formatting | bytes 1048576

commit v6 on v5

--- a/solution.py
+++ b/solution.py
@@ -37,7 +37,7 @@
     return tuple(n * 128 for n in thirds(first) + thirds(second))
 
 
-def moe_kernel(widths, fdim, f_tile, x_ref, ids_ref, gates_ref, w1_hbm, w3_hbm, w2_hbm, y_ref, *scr):
+def moe_kernel(widths, fdim, f_tile, x_hbm, ids_hbm, gates_hbm, w1_hbm, w3_hbm, w2_hbm, y_hbm, *scr):
     it = iter(scr)
     take = lambda n: [next(it) for _ in range(n)]
     gat, til, rec = take(NQ), take(NQ), take(NQ)
@@ -45,7 +45,11 @@
     pas3, pas4, pas5 = take(NQ), take(NQ), take(NQ)
     part, prec, pas6 = take(NQ), take(NQ), take(NQ)
     w1, w3, w2, act, meta_ref = take(5)
-    send_sem, recv_sem, w_sem, credit = take(4)
+    x_ref, ids_ref, gates_ref, y_ref = take(4)
+    send_sem, recv_sem, w_sem, in_sem, out_sem, credit = take(6)
+    loads = [pltpu.make_async_copy(s, d, in_sem.at[i]) for i, (s, d) in enumerate(((ids_hbm, ids_ref), (gates_hbm, gates_ref), (x_hbm, x_ref)))]
+    for c in loads:
+        c.start()
 
     offs = [sum(widths[:q]) for q in range(NQ)]
     ez, ey, ex = lax.axis_index('ez'), lax.axis_index('ey'), lax.axis_index('ex')
@@ -73,8 +77,6 @@
         cp.start()
         return cp
 
-    meta_ref[0:8] = ids_ref[...].astype(F32)
-    meta_ref[8:16] = gates_ref[...]
     bar = pltpu.get_barrier_semaphore()
     npeer = 0
     for dim in range(3):
@@ -84,6 +86,11 @@
                 npeer += 1
     pl.semaphore_signal(bar, inc=1, device_id=peer(0, 0, other), device_id_type=MESH)
     w_copies = [pltpu.make_async_copy(s, d, w_sem.at[i]) for i, (s, d) in enumerate(((w1_hbm, w1), (w3_hbm, w3), (w2_hbm, w2)))]
+    for c in loads[:2]:
+        c.wait()
+    meta_ref[0:8] = ids_ref[...].astype(F32)
+    meta_ref[8:16] = gates_ref[...]
+    loads[2].wait()
     pl.semaphore_wait(bar, npeer + 1)
 
     DIRS = (1, -1)
@@ -157,13 +164,18 @@
         for i, d in enumerate(DIRS):
             row = meta[k].at[p2[k]]
             m2[k][i] = send(row, row, peer(d2[k], d, core))
+
+    def last_chunk(wave):
+        for q in wave:
+            for i, d in enumerate(DIRS):
+                f1[q][i].wait_recv()
+            for i, d in enumerate(DIRS):
+                g2[q][i][2] = send(chunk(q, 2), chunk(q, 2), peer(d2[q], d, core))
+
+    for q in W1:
+        forward2(q, 0, 0)
+    last_chunk(W1)
     first_forwards(W2)
-    for q in W1 + W2:
-        forward2(q, 0, 0)
-        for i, d in enumerate(DIRS):
-            f1[q][i].wait_recv()
-        for i, d in enumerate(DIRS):
-            g2[q][i][2] = send(chunk(q, 2), chunk(q, 2), peer(d2[q], d, core))
     for k in range(3):
         for i in range(2):
             m2[k][i].wait_recv()
@@ -213,19 +225,19 @@
 
     for k in range(3):
         onehot(k, p2[k])
-    for q in W1 + W2:
-        select(q, p2[q])
     for q in W1:
         forward2(q, 0, 1)
         forward2(q, 1, 3)
+    for q in W1:
+        select(q, p2[q])
+    for q in W1:
+        forward2(q, 1, 2)
+    for q in W2:
+        forward2(q, 0, 0)
+    last_chunk(W2)
     for k in range(3):
         mf2[k].wait_recv()
         loop(3, lambda i, k=k: onehot(k, mod(p2[k] + 1 + i)))
-    for q in W2:
-        forward2(q, 0, 1)
-        forward2(q, 1, 3)
-    for q in W1 + W2:
-        forward2(q, 1, 2)
 
     def gathered(q, near):
         if near:
@@ -307,19 +319,26 @@
     x3 = [[Leg(q, cr, core, til[q], til_block, rec[q], sub, pas3[q]) for cr in range(2)] for q in range(NQ)]
     for q in W1:
         gathered(q, True)
+    for q in W2:
+        forward2(q, 0, 1)
+        forward2(q, 1, 3)
+    for q in W2:
+        select(q, p2[q])
     for q in W1:
         gathered(q, False)
         x3[q][0].far()
+    for q in W2:
+        forward2(q, 1, 2)
+    for q in W1:
         x3[q][0].near()
+        x3[q][1].far()
     for q in W2:
         gathered(q, True)
+    for q in W1:
+        x3[q][0].forward()
     for q in W2:
         gathered(q, False)
         x3[q][0].far()
-    for q in W1:
-        x3[q][1].far()
-    for q in W1:
-        x3[q][0].forward()
     for q in W2:
         x3[q][0].near()
         x3[q][1].far()
@@ -484,7 +503,7 @@
                     acc = acc + jnp.dot(comb[k][i, c, t], o, preferred_element_type=F32)
             part[q][i] = acc
 
-        loop(4, step)
+        return step
 
     def far6(q):
         for i, d in enumerate(DIRS):
@@ -510,22 +529,35 @@
         total = part[q][p2[q]] + prec[q][0] + prec[q][1]
         xk = x_ref[:, :, :, offs[q]:offs[q] + widths[q]].reshape(TOK, widths[q]).astype(F32)
         y_ref[:, offs[q]:offs[q] + widths[q]] = (xk + total).astype(BF16)
-
-    for q in W1:
-        combine(q)
+        cols = pl.ds(offs[q], widths[q])
+        out = pltpu.make_async_copy(y_ref.at[:, cols], y_hbm.at[:, cols], out_sem.at[q])
+        out.start()
+        return out
+
+    def far_sum(q):
+        step = combine(q)
+        step(mod(p2[q] + 2))
         far6(q)
+        return step
+
+    steps = {}
+    for q in W1:
+        steps[q] = far_sum(q)
+    for q in W1:
+        loop(3, lambda i, q=q: steps[q](mod(p2[q] + 3 + i)))
         near6(q)
     for q in W2:
-        combine(q)
-        far6(q)
+        steps[q] = far_sum(q)
     for q in W1:
         forward6(q)
     for q in W2:
+        loop(3, lambda i, q=q: steps[q](mod(p2[q] + 3 + i)))
         near6(q)
     for q in W2:
         forward6(q)
-    for q in W1 + W2:
-        final(q)
+    outs = [final(q) for q in W1 + W2]
+    for c in outs:
+        c.wait()
     for q in range(NQ):
         for cr in range(2):
             x4[q][cr].sent()
@@ -562,20 +594,25 @@
             pltpu.VMEM((fdim, hid), BF16),
             pltpu.VMEM((2, 2 * RING * RING * CAP, fdim), BF16),
             pltpu.VMEM((16, TOK), F32),
+            pltpu.VMEM(x4.shape, BF16),
+            pltpu.VMEM((8, TOK), jnp.int32),
+            pltpu.VMEM((8, TOK), F32),
+            pltpu.VMEM((tok, hid), BF16),
             pltpu.SemaphoreType.DMA((N_COPIES,)),
             pltpu.SemaphoreType.DMA((N_COPIES,)),
             pltpu.SemaphoreType.DMA((3,)),
+            pltpu.SemaphoreType.DMA((3,)),
+            pltpu.SemaphoreType.DMA((NQ,)),
             pltpu.SemaphoreType.REGULAR((3, 2)),
         ]
-        vm = pl.BlockSpec(memory_space=pltpu.VMEM)
         hbm = pl.BlockSpec(memory_space=pl.ANY)
         return pl.pallas_call(
             functools.partial(moe_kernel, widths, fdim, f_tile),
             out_shape=jax.ShapeDtypeStruct((tok, hid), BF16),
-            in_specs=[vm, vm, vm, hbm, hbm, hbm],
-            out_specs=vm,
+            in_specs=[hbm] * 6,
+            out_specs=hbm,
             scratch_shapes=scratch,
-            compiler_params=pltpu.CompilerParams(collective_id=0, has_side_effects=True, vmem_limit_bytes=67043328),
+            compiler_params=pltpu.CompilerParams(collective_id=0, has_side_effects=True, vmem_limit_bytes=62914560),
             name='moe',
         )(x4, ids_loc.T, gates_loc.T, w_g[0], w_u[0], w_d[0])
 

time: 164 us -> 157 us (0.957)
  Pallas kernels: 161 us -> 154 us
    pallas_call x1, Pallas kernels: 161 us -> 154 us  [local_layer(): pl.pallas_call(functools.partial(moe_kernel, widths, fdim, f_tile), out_s...]
where the time goes in v6:
time: 157 us; the launch traced here: 156 us
  Pallas kernels  154 us (98%)
  local copies, waits for them, and re-layouts  1.88 us (1%)
    pallas_call x1, Pallas kernels, local_layer(): pl.pallas_call(functools.partial(moe_kernel, widths, fdim, f_tile), out_s...  154 us

profile of v6, /device:TPU:1, one launch (start us, length us, event | category | flops | bytes accessed | tf_op | source)
XLA Modules:
  0.0 156.1 jit_solution(13833442990786341764)
XLA Ops:
  0.0 154.2 %moe.1 = bf16[128,2048]{1,0:T(8,128)(2,1)} custom-call(bf16[2,4,16,2048]{3,2,1,0:T(8,128)(2,1)} %bitcast.9, s32[8,128]{1,0:T(8,128)} %bitcast.10, f32[8,128]{1,0:T(8,128)} %bitcast.11, bf16[2048,768]{1,0:T(8,128)(2,1)} %bitcast.6, bf16[2048,768]{1,0:T(8,128)(2,1)} %bitcast.7, bf16[768,2048]{1,0:T(8,128)(2,1)} %bitcast.8), custom_call_target="tpu_custom_call" | custom-call | tf_op jit(solution)/shard_map/moe/pallas_call | solution.py:609
  154.2 1.9 %copy.8 = bf16[128,2048]{1,0:T(8,128)(2,1)} copy(bf16[128,2048]{1,0:T(8,128)(2,1)} %moe.1) | data formatting | bytes 1048576

commit v7 on v6

--- a/solution.py
+++ b/solution.py
@@ -12,6 +12,7 @@
 MESH = pl.DeviceIdType.MESH
 F32 = jnp.float32
 BF16 = jnp.bfloat16
+BF16_MAX = float(jnp.finfo(jnp.bfloat16).max)
 
 Z, Y, X = 0, 1, 2
 D1 = (Y, Z, X)
@@ -31,7 +32,7 @@
 
 def split_width(hid):
     tiles = hid // 128
-    second = tiles * 3 // 8
+    second = tiles * 7 // 16
     first = tiles - second
     thirds = lambda n: [n - 2 * (n // 3), n // 3, n // 3]
     return tuple(n * 128 for n in thirds(first) + thirds(second))
@@ -423,7 +424,7 @@
         rm = rank_of(jnp.concatenate(ms, axis=0))
         for b in range(4):
             hot = jnp.where(rm[b * 8:(b + 1) * 8][:, None, :] == slot, gs[b][:, None, :], 0.0).reshape(TOK, TOK).T
-            hi = hot.astype(BF16)
+            hi = jnp.minimum(hot, BF16_MAX).astype(BF16)
             r1 = hot - hi.astype(F32)
             mid = r1.astype(BF16)
             lo = (r1 - mid.astype(F32)).astype(BF16)

time: 157 us -> 155 us (0.987)
  no operation moved by 1% of the time
where the time goes in v7:
time: 155 us
  Pallas kernels  153 us (99%)
  local copies, waits for them, and re-layouts  1.88 us (1%)
    pallas_call x1, Pallas kernels, local_layer(): pl.pallas_call(functools.partial(moe_kernel, widths, fdim, f_tile), out_s...  153 us

profile of v7, /device:TPU:1, one launch (start us, length us, event | category | flops | bytes accessed | tf_op | source)
XLA Modules:
  0.0 155.3 jit_solution(15811035390212197547)
XLA Ops:
  0.0 153.4 %moe.1 = bf16[128,2048]{1,0:T(8,128)(2,1)} custom-call(bf16[2,4,16,2048]{3,2,1,0:T(8,128)(2,1)} %bitcast.9, s32[8,128]{1,0:T(8,128)} %bitcast.10, f32[8,128]{1,0:T(8,128)} %bitcast.11, bf16[2048,768]{1,0:T(8,128)(2,1)} %bitcast.6, bf16[2048,768]{1,0:T(8,128)(2,1)} %bitcast.7, bf16[768,2048]{1,0:T(8,128)(2,1)} %bitcast.8), custom_call_target="tpu_custom_call" | custom-call | tf_op jit(solution)/shard_map/moe/pallas_call | solution.py:610
  153.4 1.9 %copy.8 = bf16[128,2048]{1,0:T(8,128)(2,1)} copy(bf16[128,2048]{1,0:T(8,128)(2,1)} %moe.1) | data formatting | bytes 1048576

commit v8 on v7

--- a/solution.py
+++ b/solution.py
@@ -332,7 +332,6 @@
         forward2(q, 1, 2)
     for q in W1:
         x3[q][0].near()
-        x3[q][1].far()
     for q in W2:
         gathered(q, True)
     for q in W1:
@@ -342,15 +341,16 @@
         x3[q][0].far()
     for q in W2:
         x3[q][0].near()
+    for q in W1:
         x3[q][1].far()
     for q in W2:
         x3[q][0].forward()
+    for q in W2:
+        x3[q][1].far()
     for q in W1 + W2:
         x3[q][1].near()
     for q in W1 + W2:
         keep3(q)
-    for q in W1 + W2:
-        x3[q][1].forward()
     for c in w_copies:
         c.wait()
 
@@ -380,7 +380,11 @@
                     til[q][c, pl.ds(2 * i, 2)] = part_q.reshape(2, RING, RING, CAP, widths[q])
             loop(2, step)
 
-        loop(2, hidden)
+        hidden(0)
+        if cr == 0:
+            for q in W1 + W2:
+                x3[q][1].forward()
+        hidden(1)
         if cr == 1:
             for q in W1 + W2:
                 x4[q][0].forward()

time: 155 us -> 154 us (level)
  no operation moved by 1% of the time
where the time goes in v8:
time: 154 us
  Pallas kernels  152 us (99%)
  local copies, waits for them, and re-layouts  1.88 us (1%)
    pallas_call x1, Pallas kernels, local_layer(): pl.pallas_call(functools.partial(moe_kernel, widths, fdim, f_tile), out_s...  152 us

profile of v8, /device:TPU:1, one launch (start us, length us, event | category | flops | bytes accessed | tf_op | source)
XLA Modules:
  0.0 154.2 jit_solution(115167829877211331)
XLA Ops:
  0.0 152.4 %moe.1 = bf16[128,2048]{1,0:T(8,128)(2,1)} custom-call(bf16[2,4,16,2048]{3,2,1,0:T(8,128)(2,1)} %bitcast.9, s32[8,128]{1,0:T(8,128)} %bitcast.10, f32[8,128]{1,0:T(8,128)} %bitcast.11, bf16[2048,768]{1,0:T(8,128)(2,1)} %bitcast.6, bf16[2048,768]{1,0:T(8,128)(2,1)} %bitcast.7, bf16[768,2048]{1,0:T(8,128)(2,1)} %bitcast.8), custom_call_target="tpu_custom_call" | custom-call | tf_op jit(solution)/shard_map/moe/pallas_call | solution.py:614
  152.4 1.9 %copy.8 = bf16[128,2048]{1,0:T(8,128)(2,1)} copy(bf16[128,2048]{1,0:T(8,128)(2,1)} %moe.1) | data formatting | bytes 1048576

commit v9 on v8

--- a/solution.py
+++ b/solution.py
@@ -238,7 +238,7 @@
     last_chunk(W2)
     for k in range(3):
         mf2[k].wait_recv()
-        loop(3, lambda i, k=k: onehot(k, mod(p2[k] + 1 + i)))
+    loop(3, lambda i: [onehot(k, mod(p2[k] + 1 + i)) for k in range(3)])
 
     def gathered(q, near):
         if near:
@@ -439,8 +439,7 @@
 
     for q in W2:
         x4[q][1].forward()
-    for k in range(3):
-        loop(4, lambda i, k=k: weights(k, i))
+    loop(4, lambda i: [weights(k, i) for k in range(3)])
 
     def from_src(ref, q, d, half=None):
         cs = slice(None) if half is None else half
@@ -548,15 +547,15 @@
     steps = {}
     for q in W1:
         steps[q] = far_sum(q)
-    for q in W1:
-        loop(3, lambda i, q=q: steps[q](mod(p2[q] + 3 + i)))
+    loop(3, lambda i: [steps[q](mod(p2[q] + 3 + i)) for q in W1])
+    for q in W1:
         near6(q)
     for q in W2:
         steps[q] = far_sum(q)
     for q in W1:
         forward6(q)
-    for q in W2:
-        loop(3, lambda i, q=q: steps[q](mod(p2[q] + 3 + i)))
+    loop(3, lambda i: [steps[q](mod(p2[q] + 3 + i)) for q in W2])
+    for q in W2:
         near6(q)
     for q in W2:
         forward6(q)

time: 154 us -> 154 us (level)
  no operation moved by 1% of the time
where the time goes in v9:
time: 154 us
  Pallas kernels  152 us (99%)
  local copies, waits for them, and re-layouts  1.88 us (1%)
    pallas_call x1, Pallas kernels, local_layer(): pl.pallas_call(functools.partial(moe_kernel, widths, fdim, f_tile), out_s...  152 us

profile of v9, /device:TPU:1, one launch (start us, length us, event | category | flops | bytes accessed | tf_op | source)
XLA Modules:
  0.0 153.8 jit_solution(3506753297830846046)
XLA Ops:
  0.0 151.9 %moe.1 = bf16[128,2048]{1,0:T(8,128)(2,1)} custom-call(bf16[2,4,16,2048]{3,2,1,0:T(8,128)(2,1)} %bitcast.9, s32[8,128]{1,0:T(8,128)} %bitcast.10, f32[8,128]{1,0:T(8,128)} %bitcast.11, bf16[2048,768]{1,0:T(8,128)(2,1)} %bitcast.6, bf16[2048,768]{1,0:T(8,128)(2,1)} %bitcast.7, bf16[768,2048]{1,0:T(8,128)(2,1)} %bitcast.8), custom_call_target="tpu_custom_call" | custom-call | tf_op jit(solution)/shard_map/moe/pallas_call | solution.py:613
  152.0 1.9 %copy.8 = bf16[128,2048]{1,0:T(8,128)(2,1)} copy(bf16[128,2048]{1,0:T(8,128)(2,1)} %moe.1) | data formatting | bytes 1048576

commit v10 on v9

--- a/solution.py
+++ b/solution.py
@@ -351,63 +351,6 @@
         x3[q][1].near()
     for q in W1 + W2:
         keep3(q)
-    for c in w_copies:
-        c.wait()
-
-    x4 = [[Leg(q, cr, core if cr == 0 else other, til[q], sub, gat[q], til_block, pas4[q]) for cr in range(2)] for q in range(NQ)]
-    rows = 2 * RING * RING * CAP
-    for cr in range(2):
-        c = core if cr == 0 else other
-        for q in range(NQ):
-            x3[q][cr].arrive()
-        for q in range(NQ):
-            x3[q][cr].sent()
-
-        def hidden(i, c=c):
-            xs = jnp.concatenate([rec[q][c, pl.ds(2 * i, 2)].reshape(rows, widths[q]) for q in range(NQ)], axis=1)
-            for f in range(fdim // f_tile):
-                cols = slice(f * f_tile, (f + 1) * f_tile)
-                hg = jnp.dot(xs, w1[:, cols], preferred_element_type=F32)
-                hu = jnp.dot(xs, w3[:, cols], preferred_element_type=F32)
-                act[i, :, cols] = (hg * jax.nn.sigmoid(hg) * hu).astype(BF16)
-
-        def down(wave, c=c):
-            def step(i):
-                lo, hi = offs[wave[0]], offs[wave[-1]] + widths[wave[-1]]
-                o = jnp.dot(act[i], w2[:, lo:hi], preferred_element_type=F32).astype(BF16)
-                for q in wave:
-                    part_q = o[:, offs[q] - lo:offs[q] - lo + widths[q]]
-                    til[q][c, pl.ds(2 * i, 2)] = part_q.reshape(2, RING, RING, CAP, widths[q])
-            loop(2, step)
-
-        hidden(0)
-        if cr == 0:
-            for q in W1 + W2:
-                x3[q][1].forward()
-        hidden(1)
-        if cr == 1:
-            for q in W1 + W2:
-                x4[q][0].forward()
-        down(W1)
-        for q in W1:
-            x4[q][cr].far()
-        for q in W1:
-            x4[q][cr].near()
-        down(W2)
-        for q in W2:
-            x4[q][cr].far()
-        if cr == 1:
-            for q in W1:
-                x4[q][1].forward()
-        for q in W2:
-            x4[q][cr].near()
-        if cr == 0:
-            for q in W1 + W2:
-                keep4(q)
-    for k in range(3):
-        for i, d in enumerate(DIRS):
-            pl.semaphore_signal(credit.at[k, i], inc=1, device_id=peer(D1[k], d, core), device_id_type=MESH)
-
     def weights(k, i):
         mrow = meta[k][i, p1[k]]
         ids, gates = mrow[0:8], mrow[8:16]
@@ -437,9 +380,66 @@
             comb[k][i, b // 2, 1, :, at] = mid
             comb[k][i, b // 2, 2, :, at] = lo
 
+    loop(4, lambda i: [weights(k, i) for k in range(3)])
+    for c in w_copies:
+        c.wait()
+
+    x4 = [[Leg(q, cr, core if cr == 0 else other, til[q], sub, gat[q], til_block, pas4[q]) for cr in range(2)] for q in range(NQ)]
+    rows = 2 * RING * RING * CAP
+    for cr in range(2):
+        c = core if cr == 0 else other
+        for q in range(NQ):
+            x3[q][cr].arrive()
+        for q in range(NQ):
+            x3[q][cr].sent()
+
+        def hidden(i, c=c):
+            xs = jnp.concatenate([rec[q][c, pl.ds(2 * i, 2)].reshape(rows, widths[q]) for q in range(NQ)], axis=1)
+            for f in range(fdim // f_tile):
+                cols = slice(f * f_tile, (f + 1) * f_tile)
+                hg = jnp.dot(xs, w1[:, cols], preferred_element_type=F32)
+                hu = jnp.dot(xs, w3[:, cols], preferred_element_type=F32)
+                act[i, :, cols] = (hg * jax.nn.sigmoid(hg) * hu).astype(BF16)
+
+        def down(wave, c=c):
+            def step(i):
+                lo, hi = offs[wave[0]], offs[wave[-1]] + widths[wave[-1]]
+                o = jnp.dot(act[i], w2[:, lo:hi], preferred_element_type=F32).astype(BF16)
+                for q in wave:
+                    part_q = o[:, offs[q] - lo:offs[q] - lo + widths[q]]
+                    til[q][c, pl.ds(2 * i, 2)] = part_q.reshape(2, RING, RING, CAP, widths[q])
+            loop(2, step)
+
+        hidden(0)
+        if cr == 0:
+            for q in W1 + W2:
+                x3[q][1].forward()
+        hidden(1)
+        if cr == 1:
+            for q in W1 + W2:
+                x4[q][0].forward()
+        down(W1)
+        for q in W1:
+            x4[q][cr].far()
+        for q in W1:
+            x4[q][cr].near()
+        down(W2)
+        for q in W2:
+            x4[q][cr].far()
+        if cr == 1:
+            for q in W1:
+                x4[q][1].forward()
+        for q in W2:
+            x4[q][cr].near()
+        if cr == 0:
+            for q in W1 + W2:
+                keep4(q)
+    for k in range(3):
+        for i, d in enumerate(DIRS):
+            pl.semaphore_signal(credit.at[k, i], inc=1, device_id=peer(D1[k], d, core), device_id_type=MESH)
+
     for q in W2:
         x4[q][1].forward()
-    loop(4, lambda i: [weights(k, i) for k in range(3)])
 
     def from_src(ref, q, d, half=None):
         cs = slice(None) if half is None else half

time: 154 us -> 154 us (level)
  no operation moved by 1% of the time
where the time goes in v10:
time: 154 us
  Pallas kernels  152 us (99%)
  local copies, waits for them, and re-layouts  1.88 us (1%)
    pallas_call x1, Pallas kernels, local_layer(): pl.pallas_call(functools.partial(moe_kernel, widths, fdim, f_tile), out_s...  152 us

profile of v10, /device:TPU:1, one launch (start us, length us, event | category | flops | bytes accessed | tf_op | source)
XLA Modules:
  0.0 153.8 jit_solution(8586810441266205901)
XLA Ops:
  0.0 151.9 %moe.1 = bf16[128,2048]{1,0:T(8,128)(2,1)} custom-call(bf16[2,4,16,2048]{3,2,1,0:T(8,128)(2,1)} %bitcast.9, s32[8,128]{1,0:T(8,128)} %bitcast.10, f32[8,128]{1,0:T(8,128)} %bitcast.11, bf16[2048,768]{1,0:T(8,128)(2,1)} %bitcast.6, bf16[2048,768]{1,0:T(8,128)(2,1)} %bitcast.7, bf16[768,2048]{1,0:T(8,128)(2,1)} %bitcast.8), custom_call_target="tpu_custom_call" | custom-call | tf_op jit(solution)/shard_map/moe/pallas_call | solution.py:613
  152.0 1.9 %copy.8 = bf16[128,2048]{1,0:T(8,128)(2,1)} copy(bf16[128,2048]{1,0:T(8,128)(2,1)} %moe.1) | data formatting | bytes 1048576

commit v11 on v10

--- a/solution.py
+++ b/solution.py
@@ -46,6 +46,7 @@
     pas3, pas4, pas5 = take(NQ), take(NQ), take(NQ)
     part, prec, pas6 = take(NQ), take(NQ), take(NQ)
     w1, w3, w2, act, meta_ref = take(5)
+    gates = take(3)
     x_ref, ids_ref, gates_ref, y_ref = take(4)
     send_sem, recv_sem, w_sem, in_sem, out_sem, credit = take(6)
     loads = [pltpu.make_async_copy(s, d, in_sem.at[i]) for i, (s, d) in enumerate(((ids_hbm, ids_ref), (gates_hbm, gates_ref), (x_hbm, x_ref)))]
@@ -89,8 +90,7 @@
     w_copies = [pltpu.make_async_copy(s, d, w_sem.at[i]) for i, (s, d) in enumerate(((w1_hbm, w1), (w3_hbm, w3), (w2_hbm, w2)))]
     for c in loads[:2]:
         c.wait()
-    meta_ref[0:8] = ids_ref[...].astype(F32)
-    meta_ref[8:16] = gates_ref[...]
+    meta_ref[...] = ids_ref[...].astype(F32)
     loads[2].wait()
     pl.semaphore_wait(bar, npeer + 1)
 
@@ -115,6 +115,8 @@
     mf1 = [None] * 3
     m2 = [[None, None] for _ in range(3)]
     mf2 = [None] * 3
+    gm = [[None, None] for _ in range(3)]
+    gmf = [None] * 3
     g1 = [[None, None] for _ in range(NQ)]
     f1 = [[None, None] for _ in range(NQ)]
     g2 = [[[None] * 4, [None] * 4] for _ in range(NQ)]
@@ -159,12 +161,14 @@
         gat[q][:, :, p2[q], p1[q]] = x_ref[:, :, :, offs[q]:offs[q] + widths[q]]
     for k in range(3):
         meta[k][p2[k], p1[k]] = meta_ref[...]
+        gates[k][p2[k]] = gates_ref[...]
     first_forwards(W1)
     for k in range(3):
         mf1[k].wait_recv()
         for i, d in enumerate(DIRS):
             row = meta[k].at[p2[k]]
             m2[k][i] = send(row, row, peer(d2[k], d, core))
+            gm[k][i] = send(gates_ref, gates[k].at[p2[k]], peer(d2[k], d, core))
 
     def last_chunk(wave):
         for q in wave:
@@ -180,8 +184,12 @@
     for k in range(3):
         for i in range(2):
             m2[k][i].wait_recv()
-        src = meta[k].at[mod(p2[k] - 1)]
-        mf2[k] = send(src, src, peer(d2[k], 1, core))
+        src = meta[k].at[mod(p2[k] + 1)]
+        mf2[k] = send(src, src, peer(d2[k], -1, core))
+        for i in range(2):
+            gm[k][i].wait_recv()
+        src = gates[k].at[mod(p2[k] + 1)]
+        gmf[k] = send(src, src, peer(d2[k], -1, core))
 
     tri = (lax.broadcasted_iota(jnp.int32, (TOK, TOK), 0) < lax.broadcasted_iota(jnp.int32, (TOK, TOK), 1)).astype(BF16)
     i8 = lax.broadcasted_iota(jnp.int32, (8, 1), 0)
@@ -203,7 +211,7 @@
 
     def onehot(k, i):
         evec = experts8(k)
-        rm = rank_of(jnp.concatenate([picked(meta[k][i, j, 0:8], evec) for j in range(4)], axis=0))
+        rm = rank_of(jnp.concatenate([picked(meta[k][i, j], evec) for j in range(4)], axis=0))
         for j in range(4):
             hot = (rm[j * 8:(j + 1) * 8][:, None, :] == slot).astype(F32)
             sel[k][i, j] = hot.reshape(TOK, TOK).astype(BF16)
@@ -238,6 +246,7 @@
     last_chunk(W2)
     for k in range(3):
         mf2[k].wait_recv()
+        gmf[k].wait_recv()
     loop(3, lambda i: [onehot(k, mod(p2[k] + 1 + i)) for k in range(3)])
 
     def gathered(q, near):
@@ -251,7 +260,7 @@
             select(q, mod(p2[q] + 2))
             done = g1[q] + f1[q] + g2[q][0] + g2[q][1] + f2[q]
             if q < 3:
-                done = done + m1[q] + [mf1[q]] + m2[q] + [mf2[q]]
+                done = done + m1[q] + [mf1[q]] + m2[q] + [mf2[q]] + gm[q] + [gmf[q]]
             for c in done:
                 c.wait_send()
 
@@ -352,8 +361,7 @@
     for q in W1 + W2:
         keep3(q)
     def weights(k, i):
-        mrow = meta[k][i, p1[k]]
-        ids, gates = mrow[0:8], mrow[8:16]
+        ids, gval = meta[k][i, p1[k]], gates[k][i]
         own = lpos[D2[k]] * lstr[D2[k]]
         ms, gs = [], []
         for b in range(4):
@@ -365,7 +373,7 @@
             for j in range(8):
                 hit = ids[j:j + 1, :] == evec
                 m = m + hit.astype(F32)
-                g = g + jnp.where(hit, gates[j:j + 1, :], 0.0)
+                g = g + jnp.where(hit, gval[j:j + 1, :], 0.0)
             ms.append(m)
             gs.append(g)
         rm = rank_of(jnp.concatenate(ms, axis=0))
@@ -569,7 +577,7 @@
             cp.wait_send()
 
 
-N_COPIES = 3 * 6 + NQ * (16 + 13 + 13 + 6 + 6)
+N_COPIES = 3 * 9 + NQ * (16 + 13 + 13 + 6 + 6)
 
 
 def solution(mesh):
@@ -583,7 +591,7 @@
         each = lambda f: scratch.extend(f(w) for w in widths)
         for _ in range(3):
             each(lambda w: pltpu.VMEM(LEAD + (CAP, w), BF16))
-        scratch += [pltpu.VMEM((RING, RING, 16, TOK), F32)] * 3
+        scratch += [pltpu.VMEM((RING, RING, 8, TOK), F32)] * 3
         scratch += [pltpu.VMEM((RING, RING, TOK, TOK), BF16)] * 3
         scratch += [pltpu.VMEM((RING, 2, 3, TOK, 2 * TOK), BF16)] * 3
         each(lambda w: pltpu.VMEM((2, CORES, 2, RING, CAP, w), BF16))
@@ -597,7 +605,8 @@
             pltpu.VMEM((hid, fdim), BF16),
             pltpu.VMEM((fdim, hid), BF16),
             pltpu.VMEM((2, 2 * RING * RING * CAP, fdim), BF16),
-            pltpu.VMEM((16, TOK), F32),
+            pltpu.VMEM((8, TOK), F32),
+            *[pltpu.VMEM((RING, 8, TOK), F32)] * 3,
             pltpu.VMEM(x4.shape, BF16),
             pltpu.VMEM((8, TOK), jnp.int32),
             pltpu.VMEM((8, TOK), F32),

time: 154 us -> 151 us (0.981)
  Pallas kernels: 152 us -> 149 us
    pallas_call x1, Pallas kernels: 152 us -> 149 us  [local_layer(): pl.pallas_call(functools.partial(moe_kernel, widths, fdim, f_tile), out_s...]
where the time goes in v11:
time: 151 us
  Pallas kernels  149 us (99%)
  local copies, waits for them, and re-layouts  1.88 us (1%)
    pallas_call x1, Pallas kernels, local_layer(): pl.pallas_call(functools.partial(moe_kernel, widths, fdim, f_tile), out_s...  149 us

profile of v11, /device:TPU:1, one launch (start us, length us, event | category | flops | bytes accessed | tf_op | source)
XLA Modules:
  0.0 151.0 jit_solution(17422327062178800548)
XLA Ops:
  0.0 149.1 %moe.1 = bf16[128,2048]{1,0:T(8,128)(2,1)} custom-call(bf16[2,4,16,2048]{3,2,1,0:T(8,128)(2,1)} %bitcast.9, s32[8,128]{1,0:T(8,128)} %bitcast.10, f32[8,128]{1,0:T(8,128)} %bitcast.11, bf16[2048,768]{1,0:T(8,128)(2,1)} %bitcast.6, bf16[2048,768]{1,0:T(8,128)(2,1)} %bitcast.7, bf16[768,2048]{1,0:T(8,128)(2,1)} %bitcast.8), custom_call_target="tpu_custom_call" | custom-call | tf_op jit(solution)/shard_map/moe/pallas_call | solution.py:622
  149.1 1.9 %copy.8 = bf16[128,2048]{1,0:T(8,128)(2,1)} copy(bf16[128,2048]{1,0:T(8,128)(2,1)} %moe.1) | data formatting | bytes 1048576

commit v12 on v11

--- a/solution.py
+++ b/solution.py
@@ -244,10 +244,7 @@
     for q in W2:
         forward2(q, 0, 0)
     last_chunk(W2)
-    for k in range(3):
-        mf2[k].wait_recv()
-        gmf[k].wait_recv()
-    loop(3, lambda i: [onehot(k, mod(p2[k] + 1 + i)) for k in range(3)])
+    loop(2, lambda i: [onehot(k, mod(p2[k] - 1 + 2 * i)) for k in range(3)])
 
     def gathered(q, near):
         if near:
@@ -334,6 +331,11 @@
         forward2(q, 1, 3)
     for q in W2:
         select(q, p2[q])
+    for k in range(3):
+        mf2[k].wait_recv()
+        gmf[k].wait_recv()
+    for k in range(3):
+        onehot(k, mod(p2[k] + 2))
     for q in W1:
         gathered(q, False)
         x3[q][0].far()

time: 151 us -> 151 us (level)
  no operation moved by 1% of the time
where the time goes in v12:
time: 151 us
  Pallas kernels  149 us (99%)
  local copies, waits for them, and re-layouts  1.88 us (1%)
    pallas_call x1, Pallas kernels, local_layer(): pl.pallas_call(functools.partial(moe_kernel, widths, fdim, f_tile), out_s...  149 us

profile of v12, /device:TPU:1, one launch (start us, length us, event | category | flops | bytes accessed | tf_op | source)
XLA Modules:
  0.0 151.1 jit_solution(13975511792119368522)
XLA Ops:
  0.0 149.2 %moe.1 = bf16[128,2048]{1,0:T(8,128)(2,1)} custom-call(bf16[2,4,16,2048]{3,2,1,0:T(8,128)(2,1)} %bitcast.9, s32[8,128]{1,0:T(8,128)} %bitcast.10, f32[8,128]{1,0:T(8,128)} %bitcast.11, bf16[2048,768]{1,0:T(8,128)(2,1)} %bitcast.6, bf16[2048,768]{1,0:T(8,128)(2,1)} %bitcast.7, bf16[768,2048]{1,0:T(8,128)(2,1)} %bitcast.8), custom_call_target="tpu_custom_call" | custom-call | tf_op jit(solution)/shard_map/moe/pallas_call | solution.py:624
  149.2 1.9 %copy.8 = bf16[128,2048]{1,0:T(8,128)(2,1)} copy(bf16[128,2048]{1,0:T(8,128)(2,1)} %moe.1) | data formatting | bytes 1048576
